TPU v7x, 32 devices: a whole 2x2x4 slice. The times are simulated.
32 devices in a mesh: gx: 4 (over z), gy: 4 (over x, core), gz: 2 (over y).
Axes of the slice: x: 2, y: 2, z: 4, core: 2. Of those that a mesh axis runs over, the one named last changes fastest.
Arguments:
- hidden_in: bfloat16 [2048, 4096], P(('gx', 'gy'), 'gz'), may hold values from -40 to 40
- norm_gain: float32 [4096], P('gz'), may hold values from 0.25 to 1.75
- normed_grad: bfloat16 [2048, 4096], P(('gx', 'gy'), 'gz'), may hold values from -64 to 64
- key_grad: bfloat16 [2048, 512], P(('gx', 'gy')), may hold values from -6 to 6
- weight_blocks: bfloat16 [16, 2, 520, 128], P(('gx', 'gy'), 'gz'), may hold values from -0.09375 to 0.09375
- block_count: int32 [2, 16], P('gz'), may hold values from 1 to 520, as said below
Outputs:
- hidden_grad: bfloat16 [2048, 4096], P(('gx', 'gy'), 'gz')
- weight_grad: float32 [16, 2, 520, 128], P(('gx', 'gy'), 'gz')
Inputs may be any that keep to these rules, and one draw needn't show every extreme that they name: `block_count`: each row sums to 8192; in each row the owners i * 4 to i * 4 + 3 hold together exactly the blocks i * 2048 to min((i + 1) * 2048, 8192) - 1, and one of them holds exactly 520 blocks.
All inputs are finite; a program needn't handle non-finite values.
Results may differ from a plain program's by a relative error of at most 0.0029.
Values may be sent and summed in bfloat16 or wider, within the bound.
A program may use at most 64 MiB of HBM per device.

v0:
```python
import jax
import jax.numpy as jnp
from jax import lax
from jax.sharding import PartitionSpec as P

EPS = 1e-06


def block_layout(counts, blocks, owners, most):
    ends = jnp.cumsum(counts)
    starts = ends - counts
    block_ids = jnp.arange(blocks, dtype=jnp.int32)
    owner = jnp.searchsorted(ends, block_ids, side="right")
    gather_index = owner * most + block_ids - starts[owner]
    slot_owner = jnp.arange(owners * most, dtype=jnp.int32) // most
    slot_within = jnp.arange(owners * most, dtype=jnp.int32) % most
    valid = slot_within < counts[slot_owner]
    source = jnp.clip(starts[slot_owner] + slot_within, 0, blocks - 1)
    return (gather_index, source, valid)


def select_rows(index, keep, rows):
    columns = jnp.arange(rows.shape[0], dtype=jnp.int32)
    onehot = (index[:, None] == columns[None, :]) & keep[:, None]
    if rows.dtype == jnp.bfloat16:
        picked = jnp.dot(onehot.astype(jnp.bfloat16), rows, preferred_element_type=jnp.float32)
        return picked.astype(jnp.bfloat16)
    return jnp.dot(
        onehot.astype(jnp.float32),
        rows,
        precision=lax.Precision.HIGHEST,
        preferred_element_type=jnp.float32,
    )


def select_groups(index, keep, rows):

    def one_group(items):
        return select_rows(items[0], items[1], items[2])

    return lax.map(one_group, (index, keep, rows))


def shards(hidden_in, norm_gain, normed_grad, key_grad, weight_blocks, block_count):
    outer_size = lax.axis_size("gx")
    inner_size = lax.axis_size("gy")
    owners = outer_size * inner_size
    most = weight_blocks.shape[2]
    group_slots_count = inner_size * most
    group_rows = hidden_in.shape[1]
    width = key_grad.shape[1]
    blocks = group_rows * width // 128
    group_blocks = (blocks + outer_size - 1) // outer_size
    model_width = group_rows * lax.axis_size("gz")
    gather_index, source, valid = block_layout(block_count[0], blocks, owners, most)
    outer_index = lax.axis_index("gx")
    padded_index = jnp.pad(gather_index, (0, outer_size * group_blocks - blocks), mode="edge")
    group_offsets = jnp.arange(outer_size, dtype=jnp.int32)[:, None]
    local_index = jnp.clip(
        padded_index.reshape(outer_size, group_blocks) - group_offsets * group_slots_count,
        0,
        group_slots_count - 1,
    )
    local_source = jnp.clip(
        source.reshape(outer_size, group_slots_count) - group_offsets * group_blocks,
        0,
        group_blocks - 1,
    )
    local_valid = valid.reshape(outer_size, group_slots_count)
    all_rows = jnp.ones((outer_size, group_blocks), dtype=bool)
    local_blocks = weight_blocks.reshape(most, 128)
    gathered = lax.all_gather(local_blocks, ("gx", "gy"), axis=0, tiled=True)
    dense = select_groups(
        local_index, all_rows, gathered.reshape(outer_size, group_slots_count, 128)
    )
    weight = dense.reshape(outer_size * group_blocks, 128)[:blocks].reshape(group_rows, width)
    hfloat = hidden_in.astype(jnp.float32)
    squares = lax.psum(jnp.sum(hfloat * hfloat, axis=1), "gz")
    rstd = lax.rsqrt(squares / model_width + EPS)
    normed = (hfloat * rstd[:, None] * norm_gain).astype(jnp.bfloat16)
    dnorm = normed_grad.astype(jnp.float32) + lax.dot_general(
        key_grad, weight, (((1,), (1,)), ((), ())), preferred_element_type=jnp.float32
    )
    proj = lax.psum(jnp.sum(norm_gain * dnorm * hfloat, axis=1), "gz")
    grad = norm_gain * dnorm * rstd[:, None] - hfloat * (rstd**3 * proj / model_width)[:, None]
    hidden_grad = grad.astype(jnp.bfloat16)
    dweight = lax.dot_general(
        normed, key_grad, (((0,), (0,)), ((), ())), preferred_element_type=jnp.float32
    )
    flat = dweight.reshape(blocks, 128)
    flat_padded = jnp.pad(flat, ((0, outer_size * group_blocks - blocks), (0, 0)))
    group_sum = lax.psum_scatter(flat_padded, "gx", scatter_dimension=0, tiled=True)
    slot_source = lax.dynamic_index_in_dim(local_source, outer_index, 0, keepdims=False)
    slot_valid = lax.dynamic_index_in_dim(local_valid, outer_index, 0, keepdims=False)
    slotted = select_rows(slot_source, slot_valid, group_sum)
    owned = lax.psum_scatter(slotted, "gy", scatter_dimension=0, tiled=True)
    return (hidden_grad, owned.reshape(1, 1, most, 128))


def solution(mesh):
    placed = (
        P(("gx", "gy"), "gz"),
        P("gz"),
        P(("gx", "gy"), "gz"),
        P(("gx", "gy"), None),
        P(("gx", "gy"), "gz", None, None),
        P("gz", None),
    )
    return jax.shard_map(
        shards,
        mesh=mesh,
        in_specs=placed,
        out_specs=(P(("gx", "gy"), "gz"), P(("gx", "gy"), "gz", None, None)),
        check_vma=False,
    )
```

profile of v0, /device:TPU:0, one launch (start us, length us, event | category | flops | bytes accessed | tf_op | source)
XLA Modules:
  0.0 235.7 jit_solution(7891955440732720645)
XLA Ops:
  7.2 0.7 all-gather.3.cloned.1.call-update
  8.0 1.3 copy.18
  9.3 0.7 copy.17
  10.2 0.7 bitcast_subtract_fusion
  10.9 0.7 fusion.41
  11.6 53.5 %while.35 = (s32[]{:T(128)}, u32[8192]{0:T(1024)S(1)}, u32[8192]{0:T(1024)S(1)}, s32[16]{0:T(128)S(1)}, s32[]{:T(128)}, /*index=5*/s32[]{:T(128)}) while((s32[]{:T(128)}, u32[8192]{0:T(1024)S(1)}, u32[8192]{0:T(1024)S(1)}, s32[16]{0:T(128)S(1)}, s32[]{:T(128)}, /*index=5*/s32[]{:T(128)}) %tuple.103), condition=%wide.region_2.3_spmd.clone, body=%wide.region_1.2_spmd.clone.sunk | while | flops 311299 | bytes 131351 | solution.py:13
  11.6 0.7 fusion.52
  12.3 10.0 %fusion.53 = (u32[8192]{0:T(1024)S(1)}, u32[8192]{0:T(1024)S(1)}) fusion(u32[8192]{0:T(1024)S(1)} %get-tuple-element.281, u32[8192]{0:T(1024)S(1)} %get-tuple-element.280, s32[]{:T(128)} %bitcast.94, s32[]{:T(128)} %bitcast.95, s32[]{:T(128)} %bitcast.96, s32[]{:T(128)} %bitcast.97, s32[]{:T(128)} %bitcast.98, s32[]{:T(128)} %bitcast.99, ...), kind=kLoop, calls=%fused_computation.12.clone.1 | loop fusion | flops 311296 | bytes 131137 | tf_op jit(solution)/shard_map/jit(searchsorted)/jit(_searchsorted_scan_impl)/vmap(jit(_searchsorted_scan_impl))/while/body/eval_jaxpr/select_n | solution.py:13
  22.3 0.7 fusion.52
  23.0 10.0 %fusion.53 = (u32[8192]{0:T(1024)S(1)}, u32[8192]{0:T(1024)S(1)}) fusion(u32[8192]{0:T(1024)S(1)} %get-tuple-element.281, u32[8192]{0:T(1024)S(1)} %get-tuple-element.280, s32[]{:T(128)} %bitcast.94, s32[]{:T(128)} %bitcast.95, s32[]{:T(128)} %bitcast.96, s32[]{:T(128)} %bitcast.97, s32[]{:T(128)} %bitcast.98, s32[]{:T(128)} %bitcast.99, ...), kind=kLoop, calls=%fused_computation.12.clone.1 | loop fusion | flops 311296 | bytes 131137 | tf_op jit(solution)/shard_map/jit(searchsorted)/jit(_searchsorted_scan_impl)/vmap(jit(_searchsorted_scan_impl))/while/body/eval_jaxpr/select_n | solution.py:13
  33.0 0.7 fusion.52
  33.7 10.0 %fusion.53 = (u32[8192]{0:T(1024)S(1)}, u32[8192]{0:T(1024)S(1)}) fusion(u32[8192]{0:T(1024)S(1)} %get-tuple-element.281, u32[8192]{0:T(1024)S(1)} %get-tuple-element.280, s32[]{:T(128)} %bitcast.94, s32[]{:T(128)} %bitcast.95, s32[]{:T(128)} %bitcast.96, s32[]{:T(128)} %bitcast.97, s32[]{:T(128)} %bitcast.98, s32[]{:T(128)} %bitcast.99, ...), kind=kLoop, calls=%fused_computation.12.clone.1 | loop fusion | flops 311296 | bytes 131137 | tf_op jit(solution)/shard_map/jit(searchsorted)/jit(_searchsorted_scan_impl)/vmap(jit(_searchsorted_scan_impl))/while/body/eval_jaxpr/select_n | solution.py:13
  43.7 0.7 fusion.52
  44.4 10.0 %fusion.53 = (u32[8192]{0:T(1024)S(1)}, u32[8192]{0:T(1024)S(1)}) fusion(u32[8192]{0:T(1024)S(1)} %get-tuple-element.281, u32[8192]{0:T(1024)S(1)} %get-tuple-element.280, s32[]{:T(128)} %bitcast.94, s32[]{:T(128)} %bitcast.95, s32[]{:T(128)} %bitcast.96, s32[]{:T(128)} %bitcast.97, s32[]{:T(128)} %bitcast.98, s32[]{:T(128)} %bitcast.99, ...), kind=kLoop, calls=%fused_computation.12.clone.1 | loop fusion | flops 311296 | bytes 131137 | tf_op jit(solution)/shard_map/jit(searchsorted)/jit(_searchsorted_scan_impl)/vmap(jit(_searchsorted_scan_impl))/while/body/eval_jaxpr/select_n | solution.py:13
  54.4 0.7 fusion.52
  55.1 10.0 %fusion.53 = (u32[8192]{0:T(1024)S(1)}, u32[8192]{0:T(1024)S(1)}) fusion(u32[8192]{0:T(1024)S(1)} %get-tuple-element.281, u32[8192]{0:T(1024)S(1)} %get-tuple-element.280, s32[]{:T(128)} %bitcast.94, s32[]{:T(128)} %bitcast.95, s32[]{:T(128)} %bitcast.96, s32[]{:T(128)} %bitcast.97, s32[]{:T(128)} %bitcast.98, s32[]{:T(128)} %bitcast.99, ...), kind=kLoop, calls=%fused_computation.12.clone.1 | loop fusion | flops 311296 | bytes 131137 | tf_op jit(solution)/shard_map/jit(searchsorted)/jit(_searchsorted_scan_impl)/vmap(jit(_searchsorted_scan_impl))/while/body/eval_jaxpr/select_n | solution.py:13
  65.1 10.2 %select_subtract_fusion = s32[8192]{0:T(1024)S(1)} fusion(u32[8192]{0:T(1024)S(1)} %get-tuple-element.89, s32[]{:T(128)} %bitcast.5, s32[]{:T(128)} %bitcast.6, s32[]{:T(128)} %bitcast.7, s32[]{:T(128)} %bitcast.8, s32[]{:T(128)} %bitcast.9, s32[]{:T(128)} %bitcast.10, s32[]{:T(128)} %bitcast.11, s32[]{:T(128)} %bitcast.12, s32[]{:T(128)} %bitcast.13, ...), kind=kLoop, calls=%fused_computation.74 | loop fusion | flops 303104 | bytes 65600 | tf_op jit(solution)/shard_map/sub | solution.py:14
  75.3 0.3 copy.16
  75.7 20.5 %while.34 = (s32[]{:T(128)}, bf16[4,2048,128]{2,1,0:T(8,128)(2,1)}, s32[4,2048]{1,0:T(4,128)S(1)}, bf16[4,2080,128]{2,1,0:T(8,128)(2,1)}, s32[]{:T(128)}) while((s32[]{:T(128)}, bf16[4,2048,128]{2,1,0:T(8,128)(2,1)}, s32[4,2048]{1,0:T(4,128)S(1)}, bf16[4,2080,128]{2,1,0:T(8,128)(2,1)}, s32[]{:T(128)}) %tuple.115), condition=%wide.region_4.5_spmd, body=%wide.region_3.4_spmd.sunk | while | flops 1095041024 | bytes 1082441 | solution.py:41
  75.8 5.1 %fusion.51 = bf16[4,2048,128]{2,1,0:T(8,128)(2,1)} fusion(bf16[4,2048,128]{2,1,0:T(8,128)(2,1)} %get-tuple-element.297, s32[]{:T(128)S(6)} %copy.32, s32[2048]{0:T(1024)S(1)} %bitcast.110, bf16[4,2080,128]{2,1,0:T(8,128)(2,1)} %get-tuple-element.304), kind=kOutput, calls=%fused_computation.6.clone.1 | convolution fusion | flops 1095041024 | bytes 1065984 | tf_op jit(solution)/shard_map/while/body/eval_jaxpr/dot_general | solution.py:26
  80.9 5.1 %fusion.51 = bf16[4,2048,128]{2,1,0:T(8,128)(2,1)} fusion(bf16[4,2048,128]{2,1,0:T(8,128)(2,1)} %get-tuple-element.297, s32[]{:T(128)S(6)} %copy.32, s32[2048]{0:T(1024)S(1)} %bitcast.110, bf16[4,2080,128]{2,1,0:T(8,128)(2,1)} %get-tuple-element.304), kind=kOutput, calls=%fused_computation.6.clone.1 | convolution fusion | flops 1095041024 | bytes 1065984 | tf_op jit(solution)/shard_map/while/body/eval_jaxpr/dot_general | solution.py:26
  86.0 5.1 %fusion.51 = bf16[4,2048,128]{2,1,0:T(8,128)(2,1)} fusion(bf16[4,2048,128]{2,1,0:T(8,128)(2,1)} %get-tuple-element.297, s32[]{:T(128)S(6)} %copy.32, s32[2048]{0:T(1024)S(1)} %bitcast.110, bf16[4,2080,128]{2,1,0:T(8,128)(2,1)} %get-tuple-element.304), kind=kOutput, calls=%fused_computation.6.clone.1 | convolution fusion | flops 1095041024 | bytes 1065984 | tf_op jit(solution)/shard_map/while/body/eval_jaxpr/dot_general | solution.py:26
  91.1 5.1 %fusion.51 = bf16[4,2048,128]{2,1,0:T(8,128)(2,1)} fusion(bf16[4,2048,128]{2,1,0:T(8,128)(2,1)} %get-tuple-element.297, s32[]{:T(128)S(6)} %copy.32, s32[2048]{0:T(1024)S(1)} %bitcast.110, bf16[4,2080,128]{2,1,0:T(8,128)(2,1)} %get-tuple-element.304), kind=kOutput, calls=%fused_computation.6.clone.1 | convolution fusion | flops 1095041024 | bytes 1065984 | tf_op jit(solution)/shard_map/while/body/eval_jaxpr/dot_general | solution.py:26
  96.2 3.1 %reshape_reshape.3 = bf16[2048,512]{1,0:T(8,128)(2,1)S(1)} reshape(bf16[4,2048,128]{2,1,0:T(8,128)(2,1)} %get-tuple-element.90) | data formatting | bytes 4194304 | tf_op jit(solution)/shard_map/reshape;reshape | solution.py:76
  99.3 1.8 fusion.19
  101.1 5.9 %all-reduce.1 = (f32[128]{0:T(128)S(1)}, f32[128]{0:T(128)S(1)}) all-reduce(f32[128]{0:T(128)S(1)} %get-tuple-element.115, f32[128]{0:T(128)S(1)} %get-tuple-element.114), channel_id=1, replica_groups=mesh['gx'=4,'gy'=4,'gz'=2] {'gz'}, use_global_device_ids=true, to_apply=%region_8.9 | all-reduce | flops 256 | bytes 2048 | tf_op jit(solution)/shard_map/psum | solution.py:84
  107.0 2.7 %fusion.25 = f32[2048,512]{1,0:T(8,128)} fusion(bf16[128,512]{1,0:T(8,128)(2,1)S(1)} %copy-done, bf16[128,2048]{0,1:T(8,128)(2,1)S(1)} %copy.18, f32[128]{0:T(128)S(1)} %get-tuple-element.168, f32[2048]{0:T(1024)S(1)} %copy-done.4), kind=kOutput, calls=%fused_computation.34 | convolution fusion | flops 269484032 | bytes 4858368 | tf_op jit(solution)/shard_map/dot_general | solution.py:87
  109.7 4.7 %reshape.119 = f32[8192,128]{1,0:T(8,128)} reshape(f32[2048,512]{1,0:T(8,128)} %fusion.25) | data formatting | bytes 8388608 | tf_op jit(solution)/shard_map/reshape | solution.py:90
  114.5 0.2 compare_reduce_fusion
  114.7 0.2 compare_reduce_fusion.1
  114.9 0.2 compare_reduce_fusion.2
  115.1 0.2 compare_reduce_fusion.3
  115.3 0.2 compare_reduce_fusion.4
  115.4 0.2 compare_reduce_fusion.5
  115.6 0.2 compare_reduce_fusion.6
  115.8 0.2 compare_reduce_fusion.7
  116.0 0.4 compare_reduce_fusion.8
  116.4 4.7 %fusion.33 = s32[8320]{0:T(1024)S(1)} fusion(s32[]{:T(128)} %bitcast.14, s32[]{:T(128)} %bitcast.15, s32[]{:T(128)} %bitcast.16, s32[]{:T(128)} %bitcast.17, s32[]{:T(128)} %bitcast.18, s32[]{:T(128)} %bitcast.20, s32[]{:T(128)} %bitcast.19), kind=kLoop, calls=%fused_computation.73 | loop fusion | flops 191360 | bytes 33308 | tf_op jit(solution)/shard_map/gather | solution.py:18
  121.1 5.7 %select_select_fusion.2 = s32[8320]{0:T(1024)S(1)} fusion(pred[8320]{0:T(1024)(128)(4,1)S(1)} %compare_reduce_fusion, pred[8320]{0:T(1024)(128)(4,1)S(1)} %compare_reduce_fusion.1, pred[8320]{0:T(1024)(128)(4,1)S(1)} %compare_reduce_fusion.2, pred[8320]{0:T(1024)(128)(4,1)S(1)} %compare_reduce_fusion.3, pred[8320]{0:T(1024)(128)(4,1)S(1)} %compare_reduce_fusion.4, ...), kind=kLoop, calls=%fused_computation.66 | loop fusion | flops 74880 | bytes 141476 | tf_op jit(solution)/shard_map/gather | solution.py:18
  126.9 0.7 fusion.40
  127.6 4.6 %fusion.32 = s32[8320]{0:T(1024)S(1)} fusion(s32[]{:T(128)} %bitcast.32, s32[]{:T(128)} %bitcast.33, s32[]{:T(128)} %bitcast.34, s32[]{:T(128)} %bitcast.35, s32[]{:T(128)} %bitcast.36, s32[]{:T(128)} %bitcast.38, s32[]{:T(128)} %bitcast.37), kind=kLoop, calls=%fused_computation.72 | loop fusion | flops 191360 | bytes 33308 | tf_op jit(solution)/shard_map/gather | solution.py:17
  132.3 5.7 %select_select_fusion.1 = s32[8320]{0:T(1024)S(1)} fusion(pred[8320]{0:T(1024)(128)(4,1)S(1)} %compare_reduce_fusion, pred[8320]{0:T(1024)(128)(4,1)S(1)} %compare_reduce_fusion.1, pred[8320]{0:T(1024)(128)(4,1)S(1)} %compare_reduce_fusion.2, pred[8320]{0:T(1024)(128)(4,1)S(1)} %compare_reduce_fusion.3, pred[8320]{0:T(1024)(128)(4,1)S(1)} %compare_reduce_fusion.4, ...), kind=kLoop, calls=%fused_computation.65 | loop fusion | flops 74880 | bytes 141476 | tf_op jit(solution)/shard_map/gather | solution.py:17
  138.1 0.6 dynamic-slice.2
  138.8 0.7 clamp_reduce_fusion
  139.5 53.7 %reduce-scatter.5.cloned.1.call-done = f32[2048,128]{1,0:T(8,128)} async-done(((f32[8192,128]{1,0:T(8,128)}), f32[2048,128]{1,0:T(8,128)}) %reduce-scatter.5.cloned.1.call-update) | async-done | bytes 1048592 | tf_op jit(solution)/shard_map/reduce_scatter | solution.py:92
  193.2 10.4 %fusion.13 = f32[2080,128]{1,0:T(8,128)} fusion(f32[2048,128]{1,0:T(8,128)} %reduce-scatter.5.cloned.1.call-done, s32[2080]{0:T(1024)S(1)} %clamp_reduce_fusion, pred[2080]{0:T(1024)(128)(4,1)S(1)} %compare_reduce_fusion.9), kind=kOutput, calls=%fused_computation.18 | convolution fusion | flops 6551633920 | bytes 2123936 | tf_op jit(solution)/shard_map/dot_general | solution.py:28
  203.8 1.0 copy.19
  204.8 24.4 %reduce-scatter.7.cloned.1.call-done = f32[520,128]{1,0:T(8,128)} async-done(((f32[2080,128]{1,0:T(8,128)}), f32[520,128]{1,0:T(8,128)}) %reduce-scatter.7.cloned.1.call-update) | async-done | bytes 266256
  (35 shorter events, 1.0 us)
Async XLA Ops:
  7.2 92.2 %copy-start = (bf16[128,512]{1,0:T(8,128)(2,1)S(1)}, bf16[128,512]{1,0:T(8,128)(2,1)}, u32[]{:S(2)}) copy-start(bf16[128,512]{1,0:T(8,128)(2,1)} %param.13) | copy-start | bytes 393220
  7.2 68.2 %copy-start.2 = (bf16[128,2048]{1,0:T(8,128)(2,1)S(1)}, bf16[128,2048]{1,0:T(8,128)(2,1)}, u32[]{:S(2)}) copy-start(bf16[128,2048]{1,0:T(8,128)(2,1)} %param.12) | copy-start | bytes 1572868
  7.2 68.5 %all-gather.3.cloned.1.call-start = ((), (), s32[]{:S(2)}) async-start(), calls=%async_computation.3 | async-start | bytes 2263040 | tf_op jit(solution)/shard_map/all_gather | solution.py:72
  7.9 185.3 %reduce-scatter.5.cloned.1.call-start = ((), (), s32[]{:S(2)}) async-start(), calls=%async_computation.2 | async-start | bytes 5242880 | tf_op jit(solution)/shard_map/reduce_scatter | solution.py:92
  96.2 3.1 %copy-start.4 = (f32[2048]{0:T(1024)S(1)}, f32[2048]{0:T(1024)}, u32[]{:S(2)}) copy-start(f32[2048]{0:T(1024)} %param.11) | copy-start | bytes 24580
  114.4 12.4 %copy-start.3 = (s32[1,16]{1,0:T(1,128)S(1)}, s32[1,16]{1,0:T(1,128)}, u32[]{:S(2)}) copy-start(s32[1,16]{1,0:T(1,128)} %param.15) | copy-start | bytes 196
  114.5 114.7 %reduce-scatter.7.cloned.1.call-start = ((), (), s32[]{:S(2)}) async-start(), calls=%async_computation.4 | async-start | bytes 1331200
  139.5 64.1 %copy-start.1 = (f32[128,2048]{0,1:T(8,128)S(1)}, f32[128,2048]{0,1:T(8,128)}, u32[]{:S(2)}) copy-start(f32[128,2048]{0,1:T(8,128)} %get-tuple-element.186) | copy-start | bytes 3145732
Sparse Core Ops, SparseCore 0:
  10.2 44.2 all-gather.2
  114.6 78.5 reduce-scatter.4
  203.7 25.4 reduce-scatter.6
where the time goes:
time: 237 us; the launch traced here: 236 us
  other arithmetic  84.5 us (36%)
  waiting for transfers between devices  78.8 us (33%)
  matrix products  35.3 us (15%)
  local copies, waits for them, and re-layouts  17 us (7%)
  between operations  14 us (6%)
  blocking collectives  5.87 us (2%)
    reduce_scatter x1, waiting for transfers between devices, shards(): lax.psum_scatter(flat_padded, 'gx', scatter_dimension=0, tiled=True)  53.7 us
    select_n x5, other arithmetic, block_layout(): owner = jnp.searchsorted(ends, block_ids, side='right')  49.8 us
    unnamed x4, waiting for transfers between devices  25.1 us
    dot_general x4, matrix products, select_rows(): jnp.dot(onehot.astype(jnp.bfloat16), rows, preferred_element_type=jnp.flo...  20.4 us
    gather x11, other arithmetic, block_layout(): source = jnp.clip(starts[slot_owner] + slot_within, 0, blocks - 1)  12.3 us
    dot_general x1, matrix products, select_rows(): jnp.dot(onehot.astype(jnp.float32), rows, precision=lax.Precision.HIGHEST...  10.4 us
    gather x2, other arithmetic, block_layout(): valid = slot_within < counts[slot_owner]  10.3 us
    sub x1, other arithmetic, block_layout(): gather_index = owner * most + block_ids - starts[owner]  10.2 us
  transfers between devices with their start and end apart: 3, of which 2 were waited for; matrix products, arithmetic and copies ran while one was open for 40% of the time, Pallas kernels for 0%

commit v1 on v0

--- a/solution.py
+++ b/solution.py
@@ -1,9 +1,272 @@
+import functools
 import jax
 import jax.numpy as jnp
 from jax import lax
+from jax.experimental import pallas as pl
+from jax.experimental.pallas import tpu as pltpu
 from jax.sharding import PartitionSpec as P
 
 EPS = 1e-06
+LANE = 128
+MESH = pl.DeviceIdType.MESH
+VMEM_BUDGET = 48 * 2**20
+
+
+def owner_windows(outer, inner, blocks, most, per_row, rows):
+    group = -(-blocks // outer)
+    lows, highs = [], []
+    for i in range(outer):
+        total = min(group, blocks - i * group)
+        for j in range(inner):
+            low = max(j, total - (inner - j) * most)
+            high = min(min(j * most, total - (inner - j)) + most, total)
+            lows.append((i * group + low) // per_row // 8 * 8)
+            highs.append(-(-(i * group + high) // per_row))
+    height = -(-max(h - l for l, h in zip(lows, highs)) // 16) * 16
+    return [min(low, rows - height) for low in lows], height
+
+
+def fast_kernel(
+    dims, windows,
+    count_ref, hidden_ref, gain_ref, ngrad_ref, key_ref, wb_ref,
+    hgrad_ref, wgrad_ref,
+    kall, nt_send, nt_recv, pt_send, pt_recv, feat, wpad, wflat, wwin, dacc, dflat,
+    sq_send, sq_recv, pj_send, pj_recv,
+    own_sem, z_send, z_recv, s1_send, s1_recv, s2_send, s2_recv, s3_send, s3_recv,
+    n_send, n_recv, p_send, p_recv, e_send, e_recv,
+):
+    outer, inner, model_width, most, per_row, height, pad = dims
+    f32, bf16 = jnp.float32, jnp.bfloat16
+    a, b, g = lax.axis_index("gx"), lax.axis_index("gy"), lax.axis_index("gz")
+    x, c = b // 2, b % 2
+    ox, oc, og = 1 - x, 1 - c, 1 - g
+    me = a * inner + b
+    tokens, rows = hidden_ref.shape
+    owners = outer * inner
+    chunks = rows // LANE
+    half = tokens // 2
+
+    def peer(rel, k):
+        px = ox if k // 2 else x
+        pc = oc if k % 2 else c
+        return lax.rem(a + rel, outer), px, pc
+
+    def remote(src, dst, send, recv, gx, gy, gz):
+        return pltpu.make_async_remote_copy(
+            src_ref=src, dst_ref=dst, send_sem=send, recv_sem=recv,
+            device_id=(gx, gy, gz), device_id_type=MESH)
+
+    pairs = [(rel, k) for rel in range(outer) for k in range(inner) if rel or k]
+    barrier = pltpu.get_barrier_semaphore()
+    for rel, k in pairs:
+        pa, px, pc = peer(rel, k)
+        pl.semaphore_signal(barrier, inc=1, device_id=(pa, px * 2 + pc, g), device_id_type=MESH)
+    pl.semaphore_signal(barrier, inc=1, device_id=(a, b, og), device_id_type=MESH)
+
+    own = [pltpu.make_async_copy(key_ref.at[pl.ds(h * half, half)], kall.at[a, c, h, x], own_sem.at[h])
+           for h in range(2)]
+    for copy in own:
+        copy.start()
+
+    squares = jnp.zeros((tokens, LANE), f32)
+    for i in range(chunks):
+        part = hidden_ref[:, i * LANE:(i + 1) * LANE].astype(f32)
+        squares = squares + part * part
+    row_sum = jnp.sum(squares, axis=1, keepdims=True)
+    sq_send[...] = jnp.broadcast_to(row_sum, (tokens, LANE)).T[0:8, :]
+    for copy in own:
+        copy.wait()
+    pl.semaphore_wait(barrier, owners)
+
+    sends = []
+
+    def start(copy):
+        copy.start()
+        sends.append(copy)
+        return copy
+
+    sq_copy = start(remote(sq_send, sq_recv, e_send.at[0], e_recv.at[0], a, b, og))
+    zc = {}
+    for rel in range(1, outer):
+        piece = kall.at[a, c, g, x]
+        zc[rel] = start(remote(piece, piece, z_send.at[rel], z_recv.at[rel],
+                               lax.rem(a - rel + outer, outer), b, g))
+    bx, bc = ox * 2 + c, x * 2 + oc
+    own_piece = kall.at[a, c, g, x]
+    step1 = {0: start(remote(own_piece, own_piece, s1_send.at[0], s1_recv.at[0], a, bx, g))}
+    step2, step3 = {}, {}
+
+    begin = jnp.int32(0)
+    window_low = jnp.int32(0)
+    count = jnp.int32(0)
+    for o in range(owners):
+        value = count_ref[0, o]
+        begin = begin + jnp.where(o < me, value, 0)
+        count = count + jnp.where(me == o, value, 0)
+        window_low = window_low + jnp.where(me == o, windows[o], 0)
+    offset = jnp.clip(begin - window_low * per_row, 0, pad)
+    flat_rows = height * per_row
+    slot = lax.broadcasted_iota(jnp.int32, (most, LANE), 0)
+    wpad[...] = jnp.zeros_like(wpad)
+    wpad[pad:pad + most, :] = jnp.where(slot < count, wb_ref[...].astype(f32), 0.0)
+    wflat[...] = wpad[pl.ds(pad - offset, flat_rows), :]
+    for i in range(per_row):
+        wwin[:, i * LANE:(i + 1) * LANE] = wflat[pl.ds(i, height, stride=per_row), :].astype(bf16)
+
+    sq_copy.wait_recv()
+    total = row_sum + jnp.broadcast_to(sq_recv[0:1, :], (tokens, LANE)).T[:, 0:1]
+    rstd = lax.rsqrt(total / model_width + EPS)
+
+    for rel in range(1, outer):
+        zc[rel].wait_recv()
+        s = lax.rem(a + rel, outer)
+        piece = kall.at[s, c, g, x]
+        to = (a, bx, g) if rel % 2 else (a, b, og)
+        step1[rel] = start(remote(piece, piece, s1_send.at[rel], s1_recv.at[rel], *to))
+
+    for i in range(chunks):
+        cols = slice(i * LANE, (i + 1) * LANE)
+        normed = hidden_ref[:, cols].astype(f32) * rstd * gain_ref[:, cols]
+        feat[cols, :] = normed.T
+    for o in range(owners):
+        nt_send[o] = feat[windows[o]:windows[o] + height, :].astype(bf16)
+    nc = {}
+    for rel, k in pairs:
+        pa, px, pc = peer(rel, k)
+        nc[rel, k] = start(remote(
+            nt_send.at[pa * inner + px * 2 + pc], nt_recv.at[me],
+            n_send.at[rel * inner + k], n_recv.at[rel * inner + k], pa, px * 2 + pc, g))
+
+    for rel in range(outer):
+        step1[rel].wait_recv()
+        s = lax.rem(a + rel, outer)
+        if rel == 0:
+            piece, to = kall.at[s, c, g, ox], (a, b, og)
+        elif rel % 2:
+            piece, to = kall.at[s, c, g], (a, b, og)
+        else:
+            piece, to = kall.at[s, c, :, x], (a, bx, g)
+        step2[rel] = start(remote(piece, piece, s2_send.at[rel], s2_recv.at[rel], *to))
+    for rel in range(outer):
+        step2[rel].wait_recv()
+        piece = kall.at[lax.rem(a + rel, outer), c]
+        step3[rel] = start(remote(piece, piece, s3_send.at[rel], s3_recv.at[rel], a, bc, g))
+
+    def keys(s, px, pc):
+        return jnp.concatenate([kall[s, pc, 0, px], kall[s, pc, 1, px]], axis=0)
+
+    pc_copies = {}
+    for rel in range(outer):
+        step3[rel].wait_recv()
+        for k in range(inner):
+            pa, px, pc = peer(rel, k)
+            to = pa * inner + px * 2 + pc
+            product = lax.dot_general(
+                wwin[...], keys(pa, px, pc), (((1,), (1,)), ((), ())),
+                preferred_element_type=f32).astype(bf16)
+            if rel == 0 and k == 0:
+                pt_recv[me] = product
+            else:
+                pt_send[to] = product
+                pc_copies[rel, k] = start(remote(
+                    pt_send.at[to], pt_recv.at[me],
+                    p_send.at[rel * inner + k], p_recv.at[rel * inner + k], pa, px * 2 + pc, g))
+
+    for rel in range(outer):
+        for k in range(inner):
+            pa, px, pc = peer(outer - rel, k)
+            source = pa * inner + px * 2 + pc
+            if rel == 0 and k == 0:
+                part = nt_send[source]
+            else:
+                nc[rel, k].wait_recv()
+                part = nt_recv[source]
+            term = jnp.dot(part, keys(pa, px, pc), preferred_element_type=f32)
+            if rel == 0 and k == 0:
+                dacc[...] = term
+            else:
+                dacc[...] += term
+    for i in range(per_row):
+        dflat[pl.ds(i, height, stride=per_row), :] = dacc[:, i * LANE:(i + 1) * LANE]
+    dflat[flat_rows:, :] = jnp.zeros((most, LANE), f32)
+    wgrad_ref[...] = jnp.where(slot < count, dflat[pl.ds(offset, most), :], 0.0)
+
+    for rel, k in pairs:
+        pc_copies[rel, k].wait_recv()
+    feat[...] = jnp.zeros_like(feat)
+    for o in range(owners):
+        feat[windows[o]:windows[o] + height, :] += pt_recv[o].astype(f32)
+    proj = jnp.zeros((tokens, LANE), f32)
+    for i in range(chunks):
+        cols = slice(i * LANE, (i + 1) * LANE)
+        gained = gain_ref[:, cols] * (ngrad_ref[:, cols].astype(f32) + feat[cols, :].T)
+        feat[cols, :] = gained
+        proj = proj + gained * hidden_ref[:, cols].astype(f32)
+    proj_sum = jnp.sum(proj, axis=1, keepdims=True)
+    pj_send[...] = jnp.broadcast_to(proj_sum, (tokens, LANE)).T[0:8, :]
+    pj_copy = start(remote(pj_send, pj_recv, e_send.at[1], e_recv.at[1], a, b, og))
+    pj_copy.wait_recv()
+    proj_all = proj_sum + jnp.broadcast_to(pj_recv[0:1, :], (tokens, LANE)).T[:, 0:1]
+    scale = rstd * rstd * rstd * proj_all / model_width
+    for i in range(chunks):
+        cols = slice(i * LANE, (i + 1) * LANE)
+        grad = feat[cols, :] * rstd - hidden_ref[:, cols].astype(f32) * scale
+        hgrad_ref[:, cols] = grad.astype(bf16)
+    for copy in sends:
+        copy.wait_send()
+
+
+def fast_plan(mesh, hidden, key, wb):
+    outer, inner, halves = (mesh.shape[n] for n in ("gx", "gy", "gz"))
+    tokens, rows, width, most = hidden.shape[0], hidden.shape[1], key.shape[1], wb.shape[2]
+    if inner != 4 or halves != 2 or tokens != LANE or rows % LANE or width % LANE or most % 8:
+        return None
+    per_row = width // LANE
+    windows, height = owner_windows(outer, inner, rows * per_row, most, per_row, rows)
+    if rows % 16 or min(windows) < 0:
+        return None
+    held = outer * inner * (tokens * width * 2 + 4 * height * tokens * 2) + 6 * tokens * rows * 4
+    if held > VMEM_BUDGET:
+        return None
+    return windows, height, per_row
+
+
+def fast_shards(mesh, plan, hidden_in, norm_gain, normed_grad, key_grad, weight_blocks, block_count):
+    windows, height, per_row = plan
+    outer, inner = mesh.shape["gx"], mesh.shape["gy"]
+    owners = outer * inner
+    tokens, rows = hidden_in.shape
+    width, most = key_grad.shape[1], weight_blocks.shape[2]
+    model_width = rows * mesh.shape["gz"]
+    flat_rows = height * per_row
+    group = -(-rows * per_row // outer)
+    pad = -(-max(
+        i * group + min(j * most, group) - windows[i * inner + j] * per_row
+        for i in range(outer) for j in range(inner)) // 8) * 8
+    dims = (outer, inner, model_width, most, per_row, height, pad)
+    f32, bf16 = jnp.float32, jnp.bfloat16
+    vmem, dma = pltpu.VMEM, pltpu.SemaphoreType.DMA
+    in_vmem = pl.BlockSpec(memory_space=pltpu.VMEM)
+    hgrad, wgrad = pl.pallas_call(
+        functools.partial(fast_kernel, dims, windows),
+        out_shape=(jax.ShapeDtypeStruct((tokens, rows), bf16), jax.ShapeDtypeStruct((most, LANE), f32)),
+        in_specs=[pl.BlockSpec(memory_space=pltpu.SMEM)] + [in_vmem] * 5,
+        out_specs=(in_vmem, in_vmem),
+        scratch_shapes=[
+            vmem((outer, 2, 2, 2, tokens // 2, width), bf16),
+            vmem((owners, height, tokens), bf16), vmem((owners, height, tokens), bf16),
+            vmem((owners, height, tokens), bf16), vmem((owners, height, tokens), bf16),
+            vmem((rows, tokens), f32),
+            vmem((pad + max(flat_rows, most), LANE), f32), vmem((flat_rows, LANE), f32),
+            vmem((height, width), bf16), vmem((height, width), f32), vmem((flat_rows + most, LANE), f32),
+            vmem((8, LANE), f32), vmem((8, LANE), f32), vmem((8, LANE), f32), vmem((8, LANE), f32),
+            dma((2,)),
+        ] + [dma((outer,))] * 8 + [dma((owners,))] * 4 + [dma((2,))] * 2,
+        compiler_params=pltpu.CompilerParams(
+            collective_id=0, has_side_effects=True, vmem_limit_bytes=VMEM_BUDGET),
+    )(block_count, hidden_in, norm_gain.reshape(1, rows), normed_grad, key_grad,
+      weight_blocks.reshape(most, LANE))
+    return hgrad, wgrad.reshape(1, 1, most, LANE)
 
 
 def block_layout(counts, blocks, owners, most):
@@ -106,8 +369,15 @@
         P(("gx", "gy"), "gz", None, None),
         P("gz", None),
     )
+
+    def body(*args):
+        plan = fast_plan(mesh, args[0], args[3], args[4])
+        if plan is None:
+            return shards(*args)
+        return fast_shards(mesh, plan, *args)
+
     return jax.shard_map(
-        shards,
+        body,
         mesh=mesh,
         in_specs=placed,
         out_specs=(P(("gx", "gy"), "gz"), P(("gx", "gy"), "gz", None, None)),

time: 237 us -> 49.3 us (0.21)
  the two profiles are of different devices: /device:TPU:0 before, /device:TPU:24 now
where the time goes in v1:
time: 49.3 us; the launch traced here: 49 us
  Pallas kernels  41.6 us (84%)
  local copies, waits for them, and re-layouts  6.73 us (14%)
  between operations  0.65 us (1%)
    pallas_call x1, Pallas kernels, fast_shards(): pl.pallas_call(functools.partial(fast_kernel, dims, windows), out_shape=(...  41.6 us
    unnamed x14, local copies, waits for them, and re-layouts  6.73 us

profile of v1, /device:TPU:24, one launch (start us, length us, event | category | flops | bytes accessed | tf_op | source)
XLA Modules:
  0.0 49.0 jit_solution(6747869951358810924)
XLA Ops:
  0.6 0.0 copy-start.5
  0.6 0.6 %copy-done.5 = s32[1,16]{1,0:T(1,128)S(1)} copy-done((s32[1,16]{1,0:T(1,128)S(1)}, s32[1,16]{1,0:T(1,128)}, u32[]{:S(2)}) %copy-start.5) | copy-done | bytes 88
  1.3 0.0 copy-start
  1.3 1.0 %copy-done = bf16[128,2048]{1,0:T(8,128)(2,1)S(1)} copy-done((bf16[128,2048]{1,0:T(8,128)(2,1)S(1)}, bf16[128,2048]{1,0:T(8,128)(2,1)}, u32[]{:S(2)}) %copy-start) | copy-done | bytes 524312
  2.3 0.0 copy-start.1
  2.3 1.0 %copy-done.1 = bf16[128,2048]{1,0:T(8,128)(2,1)S(1)} copy-done((bf16[128,2048]{1,0:T(8,128)(2,1)S(1)}, bf16[128,2048]{1,0:T(8,128)(2,1)}, u32[]{:S(2)}) %copy-start.1) | copy-done | bytes 524312
  3.4 0.0 copy-start.2
  3.4 0.9 %copy-done.2 = bf16[1,1,520,128]{3,2,1,0:T(8,128)(2,1)S(1)} copy-done((bf16[1,1,520,128]{3,2,1,0:T(8,128)(2,1)S(1)}, bf16[1,1,520,128]{3,2,1,0:T(8,128)(2,1)}, u32[]{:S(2)}) %copy-start.2) | copy-done | bytes 133144
  4.3 0.0 copy-start.3
  4.3 0.9 %copy-done.3 = bf16[128,512]{1,0:T(8,128)(2,1)S(1)} copy-done((bf16[128,512]{1,0:T(8,128)(2,1)S(1)}, bf16[128,512]{1,0:T(8,128)(2,1)}, u32[]{:S(2)}) %copy-start.3) | copy-done | bytes 131096
  5.2 0.0 copy-start.4
  5.2 0.7 %copy-done.4 = f32[2048]{0:T(1024)S(1)} copy-done((f32[2048]{0:T(1024)S(1)}, f32[2048]{0:T(1024)}, u32[]{:S(2)}) %copy-start.4) | copy-done | bytes 8216
  5.9 41.6 %shard_map.77 = (bf16[128,2048]{1,0:T(8,128)(2,1)S(1)}, f32[520,128]{1,0:T(8,128)S(1)}) custom-call(s32[1,16]{1,0:T(1,128)S(1)} %copy-done.5, bf16[128,2048]{1,0:T(8,128)(2,1)S(1)} %copy-done, f32[1,2048]{1,0:T(1,128)S(1)} %bitcast.5, bf16[128,2048]{1,0:T(8,128)(2,1)S(1)} %copy-done.1, bf16[128,512]{1,0:T(8,128)(2,1)S(1)} %copy-done.3, ...), custom_call_target="tpu_custom_call" | custom-call | tf_op jit(solution)/shard_map/pallas_call | solution.py:250
  47.5 0.8 %copy.10 = bf16[128,2048]{1,0:T(8,128)(2,1)} copy(bf16[128,2048]{1,0:T(8,128)(2,1)S(1)} %get-tuple-element.8) | data formatting | bytes 1048576
  48.3 0.7 %copy.11 = f32[1,1,520,128]{3,2,1,0:T(8,128)} copy(f32[1,1,520,128]{3,2,1,0:T(8,128)S(1)} %bitcast.3) | data formatting | bytes 532480
Async XLA Ops:
  0.6 0.7 %copy-start.5 = (s32[1,16]{1,0:T(1,128)S(1)}, s32[1,16]{1,0:T(1,128)}, u32[]{:S(2)}) copy-start(s32[1,16]{1,0:T(1,128)} %count_ref.1) | copy-start | bytes 196
  1.3 1.0 %copy-start = (bf16[128,2048]{1,0:T(8,128)(2,1)S(1)}, bf16[128,2048]{1,0:T(8,128)(2,1)}, u32[]{:S(2)}) copy-start(bf16[128,2048]{1,0:T(8,128)(2,1)} %hidden_ref.1) | copy-start | bytes 1572868
  2.3 1.0 %copy-start.1 = (bf16[128,2048]{1,0:T(8,128)(2,1)S(1)}, bf16[128,2048]{1,0:T(8,128)(2,1)}, u32[]{:S(2)}) copy-start(bf16[128,2048]{1,0:T(8,128)(2,1)} %ngrad_ref.1) | copy-start | bytes 1572868
  3.4 0.9 %copy-start.2 = (bf16[1,1,520,128]{3,2,1,0:T(8,128)(2,1)S(1)}, bf16[1,1,520,128]{3,2,1,0:T(8,128)(2,1)}, u32[]{:S(2)}) copy-start(bf16[1,1,520,128]{3,2,1,0:T(8,128)(2,1)} %param.10) | copy-start | bytes 399364
  4.3 0.9 %copy-start.3 = (bf16[128,512]{1,0:T(8,128)(2,1)S(1)}, bf16[128,512]{1,0:T(8,128)(2,1)}, u32[]{:S(2)}) copy-start(bf16[128,512]{1,0:T(8,128)(2,1)} %key_ref.1) | copy-start | bytes 393220
  5.2 0.7 %copy-start.4 = (f32[2048]{0:T(1024)S(1)}, f32[2048]{0:T(1024)}, u32[]{:S(2)}) copy-start(f32[2048]{0:T(1024)} %param.7) | copy-start | bytes 24580

commit v2 on v0

--- a/solution.py
+++ b/solution.py
@@ -1,9 +1,348 @@
+import functools
 import jax
 import jax.numpy as jnp
 from jax import lax
+from jax.experimental import pallas as pl
+from jax.experimental.pallas import tpu as pltpu
 from jax.sharding import PartitionSpec as P
 
 EPS = 1e-06
+LANE = 128
+MESH = pl.DeviceIdType.MESH
+VMEM_BUDGET = 48 * 2**20
+
+
+def owner_windows(inner, group, most, per_row):
+    lows, highs = [], []
+    for j in range(inner):
+        low = max(j, group - (inner - j) * most)
+        high = min(min(j * most, group - (inner - j)) + most, group)
+        lows.append(low // per_row // 8 * 8)
+        highs.append(-(-high // per_row))
+    height = -(-max(h - l for l, h in zip(lows, highs)) // 16) * 16
+    return [min(low, group // per_row - height) for low in lows], height
+
+
+def fast_kernel(
+    dims, windows,
+    count_ref, gain_ref, hidden_hbm, ngrad_hbm, key_hbm, wb_hbm,
+    hgrad_ref, wgrad_ref,
+    hidden_ref, ngrad_ref, wb_ref, kplane, kz, nt_send, nt_recv, pt_send, pt_recv, feat, wpad, wflat,
+    wz, dacc, dwin, drecv1, dsum, drecv2, dflat, sq_send, sq_recv, pj_send, pj_recv,
+    in_sem, w_send, w_recv, k_send, k_recv, y_send, y_recv, x_send, x_recv,
+    n_send, n_recv, p_send, p_recv, d_send, d_recv, e_send, e_recv,
+):
+    outer, inner, model_width, most, per_row, height, pad = dims
+    f32, bf16 = jnp.float32, jnp.bfloat16
+    a, b, g = lax.axis_index("gx"), lax.axis_index("gy"), lax.axis_index("gz")
+    x, c = b // 2, b % 2
+    ox, oc, og = 1 - x, 1 - c, 1 - g
+    me = a * inner + b
+    bx, bc = ox * 2 + c, x * 2 + oc
+    tokens, rows = hidden_ref.shape
+    owners = outer * inner
+    chunks = rows // LANE
+    half = tokens // 2
+    group_rows = rows // outer
+    flat_rows = height * per_row
+
+    def remote(src, dst, send, recv, gx, gy, gz):
+        return pltpu.make_async_remote_copy(
+            src_ref=src, dst_ref=dst, send_sem=send, recv_sem=recv,
+            device_id=(gx, gy, gz), device_id_type=MESH)
+
+    loads = [
+        pltpu.make_async_copy(wb_hbm, wb_ref, in_sem.at[0]),
+        pltpu.make_async_copy(hidden_hbm, hidden_ref, in_sem.at[1]),
+        pltpu.make_async_copy(key_hbm, kplane.at[c, x], in_sem.at[2]),
+        pltpu.make_async_copy(key_hbm.at[pl.ds(0, half)], kz.at[a, 0], in_sem.at[3]),
+        pltpu.make_async_copy(key_hbm.at[pl.ds(half, half)], kz.at[a, 1], in_sem.at[4]),
+        pltpu.make_async_copy(ngrad_hbm, ngrad_ref, in_sem.at[5]),
+    ]
+    for load in loads:
+        load.start()
+
+    def gy_peer(k):
+        return (ox if k // 2 else x), (oc if k % 2 else c)
+
+    barrier = pltpu.get_barrier_semaphore()
+    for rel in range(1, outer):
+        pl.semaphore_signal(barrier, inc=1, device_id=(lax.rem(a + rel, outer), b, g), device_id_type=MESH)
+    for k in range(1, inner):
+        px, pc = gy_peer(k)
+        pl.semaphore_signal(barrier, inc=1, device_id=(a, px * 2 + pc, g), device_id_type=MESH)
+    pl.semaphore_signal(barrier, inc=1, device_id=(a, b, og), device_id_type=MESH)
+
+    begin = jnp.int32(0)
+    count = jnp.int32(0)
+    for o in range(owners):
+        value = count_ref[0, o]
+        begin = begin + jnp.where(o < me, value, 0)
+        count = count + jnp.where(me == o, value, 0)
+    window_low = a * group_rows
+    for j in range(inner):
+        window_low = window_low + jnp.where(b == j, windows[j], 0)
+    offset = jnp.clip(begin - window_low * per_row, 0, pad)
+    slot = lax.broadcasted_iota(jnp.int32, (most, LANE), 0)
+    wpad[...] = jnp.zeros_like(wpad)
+    loads[0].wait()
+    wpad[pad:pad + most, :] = jnp.where(slot < count, wb_ref[...].astype(f32), 0.0)
+    wflat[...] = wpad[pl.ds(pad - offset, flat_rows), :]
+    for i in range(per_row):
+        wz[a, :, i * LANE:(i + 1) * LANE] = wflat[pl.ds(i, height, stride=per_row), :].astype(bf16)
+
+    loads[1].wait()
+    squares = jnp.zeros((tokens, LANE), f32)
+    for i in range(chunks):
+        part = hidden_ref[:, i * LANE:(i + 1) * LANE].astype(f32)
+        squares = squares + part * part
+    row_sum = jnp.sum(squares, axis=1, keepdims=True)
+    sq_send[...] = jnp.broadcast_to(row_sum, (tokens, LANE)).T[0:8, :]
+    for load in loads[2:5]:
+        load.wait()
+    pl.semaphore_wait(barrier, outer + inner - 1)
+
+    sends = []
+
+    def start(make, when=None):
+        sends.append((make, when))
+        if when is None:
+            make().start()
+        else:
+            pl.when(when)(lambda: make().start())
+
+    def right(piece, send, recv, t):
+        def make():
+            return remote(piece(a - t), piece(a - t), send.at[t], recv.at[t], a + 1, b, g)
+        start(make, (a - t >= 0) & (a + 1 < outer))
+
+    def left(piece, send, recv, t):
+        at = outer - 1 + t
+        def make():
+            return remote(piece(a + t), piece(a + t), send.at[at], recv.at[at], a - 1, b, g)
+        start(make, (a + t < outer) & (a >= 1))
+
+    def arrived(piece, send, recv, t, after=None):
+        at = outer - 1 + t
+        def from_left():
+            s = a - 1 - t
+            remote(piece(s), piece(s), send.at[t], recv.at[t], a - 1, b, g).wait_recv()
+            if after is not None:
+                after(s)
+        def from_right():
+            s = a + 1 + t
+            remote(piece(s), piece(s), send.at[at], recv.at[at], a + 1, b, g).wait_recv()
+            if after is not None:
+                after(s)
+        pl.when(a - 1 - t >= 0)(from_left)
+        pl.when(a + 1 + t < outer)(from_right)
+
+    def w_piece(s):
+        return wz.at[s]
+
+    def k_piece(s):
+        return kz.at[s, g]
+
+    def sq_copy():
+        return remote(sq_send, sq_recv, e_send.at[0], e_recv.at[0], a, b, og)
+
+    def kx_copy():
+        return remote(kplane.at[c, x], kplane.at[c, x], x_send.at[0], x_recv.at[0], a, bx, g)
+
+    def kc_copy():
+        return remote(kplane.at[c], kplane.at[c], x_send.at[1], x_recv.at[1], a, bc, g)
+
+    def y_copy(s):
+        return remote(kz.at[s, g], kz.at[s, g], y_send.at[s], y_recv.at[s], a, b, og)
+
+    start(sq_copy)
+    start(kx_copy)
+    for piece, send, recv in ((w_piece, w_send, w_recv), (k_piece, k_send, k_recv)):
+        right(piece, send, recv, 0)
+        left(piece, send, recv, 0)
+
+    sq_copy().wait_recv()
+    total = row_sum + jnp.broadcast_to(sq_recv[0:1, :], (tokens, LANE)).T[:, 0:1]
+    rstd = lax.rsqrt(total / model_width + EPS)
+    for i in range(chunks):
+        cols = slice(i * LANE, (i + 1) * LANE)
+        normed = hidden_ref[:, cols].astype(f32) * rstd * gain_ref[:, cols]
+        first = i * LANE
+        nt_send[first // group_rows, first % group_rows:first % group_rows + LANE, :] = normed.T.astype(bf16)
+
+    def n_copy(rel):
+        to = lax.rem(a + rel, outer)
+        return lambda: remote(nt_send.at[to], nt_recv.at[a], n_send.at[rel], n_recv.at[rel], to, b, g)
+
+    for rel in range(1, outer):
+        start(n_copy(rel))
+
+    def relay(t):
+        arrived(w_piece, w_send, w_recv, t)
+        if t + 1 < outer - 1:
+            right(w_piece, w_send, w_recv, t + 1)
+            left(w_piece, w_send, w_recv, t + 1)
+        arrived(k_piece, k_send, k_recv, t, lambda s: y_copy(s).start())
+        if t + 1 < outer - 1:
+            right(k_piece, k_send, k_recv, t + 1)
+            left(k_piece, k_send, k_recv, t + 1)
+
+    def p_copy(s, k):
+        px, pc = gy_peer(k)
+        return remote(pt_send.at[s, k], pt_recv.at[s, b], p_send.at[s * inner + k],
+                      p_recv.at[s * inner + k], a, px * 2 + pc, g)
+
+    def products(s):
+        for k in (2, 3, 1, 0):
+            px, pc = gy_peer(k)
+            product = lax.dot_general(
+                wz[s], kplane[pc, px], (((1,), (1,)), ((), ())), preferred_element_type=f32)
+            if k == 0:
+                pt_recv[s, b] = product
+            else:
+                pt_send[s, k] = product
+                p_copy(s, k).start()
+
+    relay(0)
+    kx_copy().wait_recv()
+    start(kc_copy)
+    kc_copy().wait_recv()
+    products(a)
+    for t in range(outer - 1):
+        if t:
+            relay(t)
+        pl.when(a - 1 - t >= 0)(functools.partial(products, a - 1 - t))
+        pl.when(a + 1 + t < outer)(functools.partial(products, a + 1 + t))
+
+    nt_recv[a] = nt_send[a]
+    for rel in range(1, outer):
+        y_copy(lax.rem(a + rel, outer)).wait_recv()
+        n_copy(rel)().wait_recv()
+    dacc[...] = jnp.dot(
+        jnp.concatenate([nt_recv[s] for s in range(outer)], axis=1),
+        kz[...].reshape(outer * tokens, kz.shape[-1]), preferred_element_type=f32)
+    for j in range(inner):
+        dwin[j % 2, j // 2] = dacc[windows[j]:windows[j] + height, :]
+
+    def dc_copy():
+        return remote(dwin.at[oc], drecv1, d_send.at[0], d_recv.at[0], a, bc, g)
+
+    def dx_copy():
+        return remote(dsum.at[ox], drecv2, d_send.at[1], d_recv.at[1], a, bx, g)
+
+    start(dc_copy)
+    dc_copy().wait_recv()
+    dsum[ox] = dwin[c, ox] + drecv1[ox]
+    start(dx_copy)
+    dsum[x] = dwin[c, x] + drecv1[x]
+
+    for rel in range(outer):
+        for k in range(1, inner):
+            p_copy(lax.rem(a + rel, outer), k).wait_recv()
+    loads[5].wait()
+    feat[...] = jnp.zeros_like(feat)
+    for s in range(outer):
+        for j in range(inner):
+            low = s * group_rows + windows[j]
+            feat[low:low + height, :] += pt_recv[s, j]
+    proj = jnp.zeros((tokens, LANE), f32)
+    for i in range(chunks):
+        cols = slice(i * LANE, (i + 1) * LANE)
+        gained = gain_ref[:, cols] * (ngrad_ref[:, cols].astype(f32) + feat[cols, :].T)
+        feat[cols, :] = gained
+        proj = proj + gained * hidden_ref[:, cols].astype(f32)
+    proj_sum = jnp.sum(proj, axis=1, keepdims=True)
+    pj_send[...] = jnp.broadcast_to(proj_sum, (tokens, LANE)).T[0:8, :]
+
+    def pj_copy():
+        return remote(pj_send, pj_recv, e_send.at[1], e_recv.at[1], a, b, og)
+
+    start(pj_copy)
+
+    dx_copy().wait_recv()
+    for i in range(per_row):
+        cols = slice(i * LANE, (i + 1) * LANE)
+        dflat[pl.ds(i, height, stride=per_row), :] = dsum[x, :, cols] + drecv2[:, cols]
+    dflat[flat_rows:, :] = jnp.zeros((most, LANE), f32)
+    wgrad_ref[...] = jnp.where(slot < count, dflat[pl.ds(offset, most), :], 0.0)
+
+    pj_copy().wait_recv()
+    proj_all = proj_sum + jnp.broadcast_to(pj_recv[0:1, :], (tokens, LANE)).T[:, 0:1]
+    scale = rstd * rstd * rstd * proj_all / model_width
+    for i in range(chunks):
+        cols = slice(i * LANE, (i + 1) * LANE)
+        grad = feat[cols, :] * rstd - hidden_ref[:, cols].astype(f32) * scale
+        hgrad_ref[:, cols] = grad.astype(bf16)
+    for make, when in sends:
+        if when is None:
+            make().wait_send()
+        else:
+            pl.when(when)(lambda make=make: make().wait_send())
+    for rel in range(outer):
+        s = lax.rem(a + rel, outer)
+        if rel:
+            y_copy(s).wait_send()
+        for k in range(1, inner):
+            p_copy(s, k).wait_send()
+
+
+def fast_plan(mesh, hidden, key, wb):
+    outer, inner, halves = (mesh.shape[n] for n in ("gx", "gy", "gz"))
+    tokens, rows, width, most = hidden.shape[0], hidden.shape[1], key.shape[1], wb.shape[2]
+    if inner != 4 or halves != 2 or tokens != LANE or width % LANE or most % 8:
+        return None
+    per_row = width // LANE
+    if rows % (outer * LANE):
+        return None
+    group = rows // outer * per_row
+    windows, height = owner_windows(inner, group, most, per_row)
+    if min(windows) < 0:
+        return None
+    held = outer * (
+        4 * tokens * width + rows // outer * (4 * tokens + 4 * width) + inner * height * tokens * 8
+        + height * width * 2) + 6 * height * width * 4 * 2 + tokens * rows * 12
+    if held > VMEM_BUDGET:
+        return None
+    return windows, height, per_row, group
+
+
+def fast_shards(mesh, plan, hidden_in, norm_gain, normed_grad, key_grad, weight_blocks, block_count):
+    windows, height, per_row, group = plan
+    outer, inner = mesh.shape["gx"], mesh.shape["gy"]
+    tokens, rows = hidden_in.shape
+    width, most = key_grad.shape[1], weight_blocks.shape[2]
+    model_width = rows * mesh.shape["gz"]
+    flat_rows = height * per_row
+    pad = -(-max(min(j * most, group - inner + j) - windows[j] * per_row for j in range(inner)) // 8) * 8
+    dims = (outer, inner, model_width, most, per_row, height, pad)
+    f32, bf16 = jnp.float32, jnp.bfloat16
+    vmem, dma = pltpu.VMEM, pltpu.SemaphoreType.DMA
+    in_vmem = pl.BlockSpec(memory_space=pltpu.VMEM)
+    in_hbm = pl.BlockSpec(memory_space=pltpu.HBM)
+    hgrad, wgrad = pl.pallas_call(
+        functools.partial(fast_kernel, dims, windows),
+        out_shape=(jax.ShapeDtypeStruct((tokens, rows), bf16), jax.ShapeDtypeStruct((most, LANE), f32)),
+        in_specs=[pl.BlockSpec(memory_space=pltpu.SMEM), in_vmem] + [in_hbm] * 4,
+        out_specs=(in_vmem, in_vmem),
+        scratch_shapes=[
+            vmem((tokens, rows), bf16), vmem((tokens, rows), bf16), vmem((most, LANE), bf16),
+            vmem((2, 2, tokens, width), bf16), vmem((outer, 2, tokens // 2, width), bf16),
+            vmem((outer, rows // outer, tokens), bf16), vmem((outer, rows // outer, tokens), bf16),
+            vmem((outer, inner, height, tokens), f32), vmem((outer, inner, height, tokens), f32),
+            vmem((rows, tokens), f32),
+            vmem((pad + max(flat_rows, most), LANE), f32), vmem((flat_rows, LANE), f32),
+            vmem((outer, height, width), bf16), vmem((rows // outer, width), f32),
+            vmem((2, 2, height, width), f32), vmem((2, height, width), f32), vmem((2, height, width), f32),
+            vmem((height, width), f32), vmem((flat_rows + most, LANE), f32),
+            vmem((8, LANE), f32), vmem((8, LANE), f32), vmem((8, LANE), f32), vmem((8, LANE), f32),
+            dma((6,)),
+        ] + [dma((2 * (outer - 1),))] * 4 + [dma((outer,))] * 2 + [dma((2,))] * 2
+        + [dma((outer,))] * 2 + [dma((outer * inner,))] * 2 + [dma((2,))] * 4,
+        compiler_params=pltpu.CompilerParams(
+            collective_id=0, has_side_effects=True, vmem_limit_bytes=VMEM_BUDGET),
+    )(block_count, norm_gain.reshape(1, rows), hidden_in, normed_grad, key_grad,
+      weight_blocks.reshape(most, LANE))
+    return hgrad, wgrad.reshape(1, 1, most, LANE)
 
 
 def block_layout(counts, blocks, owners, most):
@@ -106,8 +445,15 @@
         P(("gx", "gy"), "gz", None, None),
         P("gz", None),
     )
+
+    def body(*args):
+        plan = fast_plan(mesh, args[0], args[3], args[4])
+        if plan is None:
+            return shards(*args)
+        return fast_shards(mesh, plan, *args)
+
     return jax.shard_map(
-        shards,
+        body,
         mesh=mesh,
         in_specs=placed,
         out_specs=(P(("gx", "gy"), "gz"), P(("gx", "gy"), "gz", None, None)),

time: 237 us -> 53.1 us (0.22)
  other arithmetic: 84.5 us -> 0 us
  waiting for transfers between devices: 78.8 us -> 0 us
  Pallas kernels: 0 us -> 44.8 us
  matrix products: 35.3 us -> 0 us
  between operations: 14 us -> 0.65 us
  local copies, waits for them, and re-layouts: 17 us -> 6.73 us
  blocking collectives: 5.87 us -> 0 us
    reduce_scatter x1 -> x0, waiting for transfers between devices: 53.7 us -> none  [shards(): lax.psum_scatter(flat_padded, 'gx', scatter_dimension=0, tiled=True)]
    select_n x6 -> x0, other arithmetic: 49.8 us -> none  [the longest x5 49.8 us: block_layout(): owner = jnp.searchsorted(ends, block_ids, side='right')]
    pallas_call x0 -> x1, Pallas kernels: none -> 44.8 us  [fast_shards(): pl.pallas_call(functools.partial(fast_kernel, dims, windows), out_shape=(...]
    dot_general x7 -> x0, matrix products: 35.3 us -> none  [the longest x4 20.4 us: select_rows(): jnp.dot(onehot.astype(jnp.bfloat16), rows, preferred_element_type=jnp.flo...]
    unnamed x4 -> x0, waiting for transfers between devices: 25.1 us -> none
    gather x13 -> x0, other arithmetic: 22.6 us -> none  [the longest x11 12.3 us: block_layout(): source = jnp.clip(starts[slot_owner] + slot_within, 0, blocks - 1)]
    sub x2 -> x0, other arithmetic: 10.8 us -> none  [the longest x1 10.2 us: block_layout(): gather_index = owner * most + block_ids - starts[owner]]
    psum x1 -> x0, blocking collectives: 5.87 us -> none  [shards(): proj = lax.psum(jnp.sum(norm_gain * dnorm * hfloat, axis=1), 'gz')]
  transfers between devices with their start and end apart: 3 -> 0, of which waited for: 2 -> 0; matrix products, arithmetic and copies ran while one was open for 40% -> 0% of each run, Pallas kernels for 0% -> 0%
where the time goes in v2:
time: 53.1 us; the launch traced here: 52.1 us
  Pallas kernels  44.8 us (84%)
  local copies, waits for them, and re-layouts  6.73 us (13%)
  between operations  0.65 us (1%)
    pallas_call x1, Pallas kernels, fast_shards(): pl.pallas_call(functools.partial(fast_kernel, dims, windows), out_shape=(...  44.8 us
    unnamed x14, local copies, waits for them, and re-layouts  6.73 us

profile of v2, /device:TPU:0, one launch (start us, length us, event | category | flops | bytes accessed | tf_op | source)
XLA Modules:
  0.0 52.1 jit_solution(9425972412977605055)
XLA Ops:
  0.6 0.0 copy-start.5
  0.6 0.6 %copy-done.5 = s32[1,16]{1,0:T(1,128)S(1)} copy-done((s32[1,16]{1,0:T(1,128)S(1)}, s32[1,16]{1,0:T(1,128)}, u32[]{:S(2)}) %copy-start.5) | copy-done | bytes 88
  1.3 0.0 copy-start
  1.3 1.0 %copy-done = bf16[128,2048]{1,0:T(8,128)(2,1)S(1)} copy-done((bf16[128,2048]{1,0:T(8,128)(2,1)S(1)}, bf16[128,2048]{1,0:T(8,128)(2,1)}, u32[]{:S(2)}) %copy-start) | copy-done | bytes 524312
  2.3 0.0 copy-start.1
  2.3 1.0 %copy-done.1 = bf16[128,2048]{1,0:T(8,128)(2,1)S(1)} copy-done((bf16[128,2048]{1,0:T(8,128)(2,1)S(1)}, bf16[128,2048]{1,0:T(8,128)(2,1)}, u32[]{:S(2)}) %copy-start.1) | copy-done | bytes 524312
  3.4 0.0 copy-start.2
  3.4 0.9 %copy-done.2 = bf16[1,1,520,128]{3,2,1,0:T(8,128)(2,1)S(1)} copy-done((bf16[1,1,520,128]{3,2,1,0:T(8,128)(2,1)S(1)}, bf16[1,1,520,128]{3,2,1,0:T(8,128)(2,1)}, u32[]{:S(2)}) %copy-start.2) | copy-done | bytes 133144
  4.3 0.0 copy-start.3
  4.3 0.9 %copy-done.3 = bf16[128,512]{1,0:T(8,128)(2,1)S(1)} copy-done((bf16[128,512]{1,0:T(8,128)(2,1)S(1)}, bf16[128,512]{1,0:T(8,128)(2,1)}, u32[]{:S(2)}) %copy-start.3) | copy-done | bytes 131096
  5.2 0.0 copy-start.4
  5.2 0.7 %copy-done.4 = f32[2048]{0:T(1024)S(1)} copy-done((f32[2048]{0:T(1024)S(1)}, f32[2048]{0:T(1024)}, u32[]{:S(2)}) %copy-start.4) | copy-done | bytes 8216
  5.9 44.8 %shard_map.77 = (bf16[128,2048]{1,0:T(8,128)(2,1)S(1)}, f32[520,128]{1,0:T(8,128)S(1)}) custom-call(s32[1,16]{1,0:T(1,128)S(1)} %copy-done.5, f32[1,2048]{1,0:T(1,128)S(1)} %bitcast.5, bf16[128,2048]{1,0:T(8,128)(2,1)S(1)} %copy-done, bf16[128,2048]{1,0:T(8,128)(2,1)S(1)} %copy-done.1, bf16[128,512]{1,0:T(8,128)(2,1)S(1)} %copy-done.3, ...), custom_call_target="tpu_custom_call" | custom-call | tf_op jit(solution)/shard_map/pallas_call | solution.py:322
  50.6 0.8 %copy.10 = bf16[128,2048]{1,0:T(8,128)(2,1)} copy(bf16[128,2048]{1,0:T(8,128)(2,1)S(1)} %get-tuple-element.8) | data formatting | bytes 1048576
  51.4 0.7 %copy.11 = f32[1,1,520,128]{3,2,1,0:T(8,128)} copy(f32[1,1,520,128]{3,2,1,0:T(8,128)S(1)} %bitcast.3) | data formatting | bytes 532480
Async XLA Ops:
  0.6 0.7 %copy-start.5 = (s32[1,16]{1,0:T(1,128)S(1)}, s32[1,16]{1,0:T(1,128)}, u32[]{:S(2)}) copy-start(s32[1,16]{1,0:T(1,128)} %count_ref.1) | copy-start | bytes 196
  1.3 1.0 %copy-start = (bf16[128,2048]{1,0:T(8,128)(2,1)S(1)}, bf16[128,2048]{1,0:T(8,128)(2,1)}, u32[]{:S(2)}) copy-start(bf16[128,2048]{1,0:T(8,128)(2,1)} %hidden_hbm.1) | copy-start | bytes 1572868
  2.3 1.0 %copy-start.1 = (bf16[128,2048]{1,0:T(8,128)(2,1)S(1)}, bf16[128,2048]{1,0:T(8,128)(2,1)}, u32[]{:S(2)}) copy-start(bf16[128,2048]{1,0:T(8,128)(2,1)} %ngrad_hbm.1) | copy-start | bytes 1572868
  3.4 0.9 %copy-start.2 = (bf16[1,1,520,128]{3,2,1,0:T(8,128)(2,1)S(1)}, bf16[1,1,520,128]{3,2,1,0:T(8,128)(2,1)}, u32[]{:S(2)}) copy-start(bf16[1,1,520,128]{3,2,1,0:T(8,128)(2,1)} %param.10) | copy-start | bytes 399364
  4.3 0.9 %copy-start.3 = (bf16[128,512]{1,0:T(8,128)(2,1)S(1)}, bf16[128,512]{1,0:T(8,128)(2,1)}, u32[]{:S(2)}) copy-start(bf16[128,512]{1,0:T(8,128)(2,1)} %key_hbm.1) | copy-start | bytes 393220
  5.2 0.7 %copy-start.4 = (f32[2048]{0:T(1024)S(1)}, f32[2048]{0:T(1024)}, u32[]{:S(2)}) copy-start(f32[2048]{0:T(1024)} %param.7) | copy-start | bytes 24580

commit v3 on v2

--- a/solution.py
+++ b/solution.py
@@ -32,7 +32,7 @@
     in_sem, w_send, w_recv, k_send, k_recv, y_send, y_recv, x_send, x_recv,
     n_send, n_recv, p_send, p_recv, d_send, d_recv, e_send, e_recv,
 ):
-    outer, inner, model_width, most, per_row, height, pad = dims
+    outer, inner, model_width, most, per_row, height, pad, parts, part_rows = dims
     f32, bf16 = jnp.float32, jnp.bfloat16
     a, b, g = lax.axis_index("gx"), lax.axis_index("gy"), lax.axis_index("gz")
     x, c = b // 2, b % 2
@@ -91,6 +91,66 @@
     for i in range(per_row):
         wz[a, :, i * LANE:(i + 1) * LANE] = wflat[pl.ds(i, height, stride=per_row), :].astype(bf16)
 
+    for load in loads[2:5]:
+        load.wait()
+    pl.semaphore_wait(barrier, outer + inner - 1)
+
+    sends = []
+
+    def start(make, when=None):
+        sends.append((make, when))
+        if when is None:
+            make().start()
+        else:
+            pl.when(when)(lambda: make().start())
+
+    def right(piece, send, recv, t):
+        def make():
+            return remote(piece(a - t), piece(a - t), send.at[t], recv.at[t], a + 1, b, g)
+        start(make, (a - t >= 0) & (a + 1 < outer))
+
+    def left(piece, send, recv, t):
+        at = outer - 1 + t
+        def make():
+            return remote(piece(a + t), piece(a + t), send.at[at], recv.at[at], a - 1, b, g)
+        start(make, (a + t < outer) & (a >= 1))
+
+    def arrived(piece, send, recv, t):
+        at = outer - 1 + t
+        def from_left():
+            s = a - 1 - t
+            remote(piece(s), piece(s), send.at[t], recv.at[t], a - 1, b, g).wait_recv()
+        def from_right():
+            s = a + 1 + t
+            remote(piece(s), piece(s), send.at[at], recv.at[at], a + 1, b, g).wait_recv()
+        pl.when(a - 1 - t >= 0)(from_left)
+        pl.when(a + 1 + t < outer)(from_right)
+
+    def w_piece(s):
+        return wz.at[s]
+
+    def k_copy(rel):
+        to = lax.rem(a + rel, outer)
+        return lambda: remote(kz.at[a, g], kz.at[a, g], k_send.at[rel], k_recv.at[rel], to, b, g)
+
+    def sq_copy():
+        return remote(sq_send, sq_recv, e_send.at[0], e_recv.at[0], a, b, og)
+
+    def kx_copy():
+        return remote(kplane.at[c, x], kplane.at[c, x], x_send.at[0], x_recv.at[0], a, bx, g)
+
+    def kc_copy():
+        return remote(kplane.at[c], kplane.at[c], x_send.at[1], x_recv.at[1], a, bc, g)
+
+    def y_copy(s):
+        return remote(kz.at[s, g], kz.at[s, g], y_send.at[s], y_recv.at[s], a, b, og)
+
+    start(kx_copy)
+    right(w_piece, w_send, w_recv, 0)
+    left(w_piece, w_send, w_recv, 0)
+    for rel in range(1, outer):
+        start(k_copy(rel))
+
     loads[1].wait()
     squares = jnp.zeros((tokens, LANE), f32)
     for i in range(chunks):
@@ -98,94 +158,38 @@
         squares = squares + part * part
     row_sum = jnp.sum(squares, axis=1, keepdims=True)
     sq_send[...] = jnp.broadcast_to(row_sum, (tokens, LANE)).T[0:8, :]
-    for load in loads[2:5]:
-        load.wait()
-    pl.semaphore_wait(barrier, outer + inner - 1)
-
-    sends = []
-
-    def start(make, when=None):
-        sends.append((make, when))
-        if when is None:
-            make().start()
-        else:
-            pl.when(when)(lambda: make().start())
-
-    def right(piece, send, recv, t):
-        def make():
-            return remote(piece(a - t), piece(a - t), send.at[t], recv.at[t], a + 1, b, g)
-        start(make, (a - t >= 0) & (a + 1 < outer))
-
-    def left(piece, send, recv, t):
-        at = outer - 1 + t
-        def make():
-            return remote(piece(a + t), piece(a + t), send.at[at], recv.at[at], a - 1, b, g)
-        start(make, (a + t < outer) & (a >= 1))
-
-    def arrived(piece, send, recv, t, after=None):
-        at = outer - 1 + t
-        def from_left():
-            s = a - 1 - t
-            remote(piece(s), piece(s), send.at[t], recv.at[t], a - 1, b, g).wait_recv()
-            if after is not None:
-                after(s)
-        def from_right():
-            s = a + 1 + t
-            remote(piece(s), piece(s), send.at[at], recv.at[at], a + 1, b, g).wait_recv()
-            if after is not None:
-                after(s)
-        pl.when(a - 1 - t >= 0)(from_left)
-        pl.when(a + 1 + t < outer)(from_right)
-
-    def w_piece(s):
-        return wz.at[s]
-
-    def k_piece(s):
-        return kz.at[s, g]
-
-    def sq_copy():
-        return remote(sq_send, sq_recv, e_send.at[0], e_recv.at[0], a, b, og)
-
-    def kx_copy():
-        return remote(kplane.at[c, x], kplane.at[c, x], x_send.at[0], x_recv.at[0], a, bx, g)
-
-    def kc_copy():
-        return remote(kplane.at[c], kplane.at[c], x_send.at[1], x_recv.at[1], a, bc, g)
-
-    def y_copy(s):
-        return remote(kz.at[s, g], kz.at[s, g], y_send.at[s], y_recv.at[s], a, b, og)
-
     start(sq_copy)
-    start(kx_copy)
-    for piece, send, recv in ((w_piece, w_send, w_recv), (k_piece, k_send, k_recv)):
-        right(piece, send, recv, 0)
-        left(piece, send, recv, 0)
-
     sq_copy().wait_recv()
     total = row_sum + jnp.broadcast_to(sq_recv[0:1, :], (tokens, LANE)).T[:, 0:1]
     rstd = lax.rsqrt(total / model_width + EPS)
     for i in range(chunks):
         cols = slice(i * LANE, (i + 1) * LANE)
         normed = hidden_ref[:, cols].astype(f32) * rstd * gain_ref[:, cols]
-        first = i * LANE
-        nt_send[first // group_rows, first % group_rows:first % group_rows + LANE, :] = normed.T.astype(bf16)
-
-    def n_copy(rel):
+        turned = normed.T.astype(bf16)
+        low = i * LANE % group_rows
+        for part in range(2):
+            begins = max(low, parts[part])
+            ends = min(low + LANE, parts[part] + part_rows)
+            if begins < ends:
+                nt_send[i * LANE // group_rows, part, begins - parts[part]:ends - parts[part], :] = (
+                    turned[begins - low:ends - low, :])
+
+    def n_copy(rel, turn):
         to = lax.rem(a + rel, outer)
-        return lambda: remote(nt_send.at[to], nt_recv.at[a], n_send.at[rel], n_recv.at[rel], to, b, g)
-
-    for rel in range(1, outer):
-        start(n_copy(rel))
+        part = x if turn else ox
+        at = turn * outer + rel
+        return lambda: remote(
+            nt_send.at[to, part], nt_recv.at[a, part], n_send.at[at], n_recv.at[at], to, b, g)
+
+    for turn in range(2):
+        for rel in range(1, outer):
+            start(n_copy(rel, turn))
 
     def relay(t):
         arrived(w_piece, w_send, w_recv, t)
         if t + 1 < outer - 1:
             right(w_piece, w_send, w_recv, t + 1)
             left(w_piece, w_send, w_recv, t + 1)
-        arrived(k_piece, k_send, k_recv, t, lambda s: y_copy(s).start())
-        if t + 1 < outer - 1:
-            right(k_piece, k_send, k_recv, t + 1)
-            left(k_piece, k_send, k_recv, t + 1)
 
     def p_copy(s, k):
         px, pc = gy_peer(k)
@@ -203,38 +207,53 @@
                 pt_send[s, k] = product
                 p_copy(s, k).start()
 
-    relay(0)
+    def dc_copy(turn):
+        part = x if turn else ox
+        return lambda: remote(
+            dwin.at[part, oc], drecv1.at[part], d_send.at[turn], d_recv.at[turn], a, bc, g)
+
+    def dx_copy():
+        return remote(dsum, drecv2, d_send.at[2], d_recv.at[2], a, bx, g)
+
+    def window_sums(turn):
+        part = x if turn else ox
+        for rel in range(1, outer):
+            n_copy(rel, turn)().wait_recv()
+        nt_recv[a, part] = nt_send[a, part]
+        dacc[...] = jnp.dot(
+            jnp.concatenate([nt_recv[s, part] for s in range(outer)], axis=1),
+            kz[...].reshape(outer * tokens, kz.shape[-1]), preferred_element_type=f32)
+        for pc in range(2):
+            low = jnp.where(part == 0, windows[pc] - parts[0], windows[2 + pc] - parts[1])
+            dwin[part, pc] = dacc[pl.ds(pl.multiple_of(low, 8), height), :]
+        start(dc_copy(turn))
+
+    def products_from(t):
+        pl.when(a - 1 - t >= 0)(functools.partial(products, a - 1 - t))
+        pl.when(a + 1 + t < outer)(functools.partial(products, a + 1 + t))
+
+    for rel in range(1, outer):
+        k_copy(rel)().wait_recv()
+        s = lax.rem(a - rel + outer, outer)
+        start(functools.partial(y_copy, s))
     kx_copy().wait_recv()
     start(kc_copy)
+    relay(0)
     kc_copy().wait_recv()
     products(a)
-    for t in range(outer - 1):
-        if t:
-            relay(t)
-        pl.when(a - 1 - t >= 0)(functools.partial(products, a - 1 - t))
-        pl.when(a + 1 + t < outer)(functools.partial(products, a + 1 + t))
-
-    nt_recv[a] = nt_send[a]
+    products_from(0)
+    for t in range(1, outer - 2):
+        relay(t)
+        products_from(t)
     for rel in range(1, outer):
         y_copy(lax.rem(a + rel, outer)).wait_recv()
-        n_copy(rel)().wait_recv()
-    dacc[...] = jnp.dot(
-        jnp.concatenate([nt_recv[s] for s in range(outer)], axis=1),
-        kz[...].reshape(outer * tokens, kz.shape[-1]), preferred_element_type=f32)
-    for j in range(inner):
-        dwin[j % 2, j // 2] = dacc[windows[j]:windows[j] + height, :]
-
-    def dc_copy():
-        return remote(dwin.at[oc], drecv1, d_send.at[0], d_recv.at[0], a, bc, g)
-
-    def dx_copy():
-        return remote(dsum.at[ox], drecv2, d_send.at[1], d_recv.at[1], a, bx, g)
-
-    start(dc_copy)
-    dc_copy().wait_recv()
-    dsum[ox] = dwin[c, ox] + drecv1[ox]
+    window_sums(0)
+    dc_copy(0)().wait_recv()
+    dsum[...] = dwin[ox, c] + drecv1[ox]
     start(dx_copy)
-    dsum[x] = dwin[c, x] + drecv1[x]
+    relay(outer - 2)
+    products_from(outer - 2)
+    window_sums(1)
 
     for rel in range(outer):
         for k in range(1, inner):
@@ -259,10 +278,11 @@
 
     start(pj_copy)
 
+    dc_copy(1)().wait_recv()
     dx_copy().wait_recv()
     for i in range(per_row):
         cols = slice(i * LANE, (i + 1) * LANE)
-        dflat[pl.ds(i, height, stride=per_row), :] = dsum[x, :, cols] + drecv2[:, cols]
+        dflat[pl.ds(i, height, stride=per_row), :] = dwin[x, c, :, cols] + drecv1[x, :, cols] + drecv2[:, cols]
     dflat[flat_rows:, :] = jnp.zeros((most, LANE), f32)
     wgrad_ref[...] = jnp.where(slot < count, dflat[pl.ds(offset, most), :], 0.0)
 
@@ -280,8 +300,6 @@
             pl.when(when)(lambda make=make: make().wait_send())
     for rel in range(outer):
         s = lax.rem(a + rel, outer)
-        if rel:
-            y_copy(s).wait_send()
         for k in range(1, inner):
             p_copy(s, k).wait_send()
 
@@ -296,7 +314,7 @@
         return None
     group = rows // outer * per_row
     windows, height = owner_windows(inner, group, most, per_row)
-    if min(windows) < 0:
+    if min(windows) < 0 or rows // outer < 2 * height + 16:
         return None
     held = outer * (
         4 * tokens * width + rows // outer * (4 * tokens + 4 * width) + inner * height * tokens * 8
@@ -314,7 +332,11 @@
     model_width = rows * mesh.shape["gz"]
     flat_rows = height * per_row
     pad = -(-max(min(j * most, group - inner + j) - windows[j] * per_row for j in range(inner)) // 8) * 8
-    dims = (outer, inner, model_width, most, per_row, height, pad)
+    parts = [min(windows[0:2]), min(windows[2:4])]
+    part_rows = max(max(windows[0:2]) - parts[0], max(windows[2:4]) - parts[1]) + height
+    part_rows = -(-part_rows // 16) * 16
+    parts = [min(low, rows // outer - part_rows) for low in parts]
+    dims = (outer, inner, model_width, most, per_row, height, pad, parts, part_rows)
     f32, bf16 = jnp.float32, jnp.bfloat16
     vmem, dma = pltpu.VMEM, pltpu.SemaphoreType.DMA
     in_vmem = pl.BlockSpec(memory_space=pltpu.VMEM)
@@ -327,19 +349,19 @@
         scratch_shapes=[
             vmem((tokens, rows), bf16), vmem((tokens, rows), bf16), vmem((most, LANE), bf16),
             vmem((2, 2, tokens, width), bf16), vmem((outer, 2, tokens // 2, width), bf16),
-            vmem((outer, rows // outer, tokens), bf16), vmem((outer, rows // outer, tokens), bf16),
+            vmem((outer, 2, part_rows, tokens), bf16), vmem((outer, 2, part_rows, tokens), bf16),
             vmem((outer, inner, height, tokens), f32), vmem((outer, inner, height, tokens), f32),
             vmem((rows, tokens), f32),
             vmem((pad + max(flat_rows, most), LANE), f32), vmem((flat_rows, LANE), f32),
-            vmem((outer, height, width), bf16), vmem((rows // outer, width), f32),
-            vmem((2, 2, height, width), f32), vmem((2, height, width), f32), vmem((2, height, width), f32),
+            vmem((outer, height, width), bf16), vmem((part_rows, width), f32),
+            vmem((2, 2, height, width), f32), vmem((2, height, width), f32), vmem((height, width), f32),
             vmem((height, width), f32), vmem((flat_rows + most, LANE), f32),
             vmem((8, LANE), f32), vmem((8, LANE), f32), vmem((8, LANE), f32), vmem((8, LANE), f32),
             dma((6,)),
         ] + [dma((2 * (outer - 1),))] * 4 + [dma((outer,))] * 2 + [dma((2,))] * 2
-        + [dma((outer,))] * 2 + [dma((outer * inner,))] * 2 + [dma((2,))] * 4,
+        + [dma((2 * outer,))] * 2 + [dma((outer * inner,))] * 2 + [dma((3,))] * 2 + [dma((2,))] * 2,
         compiler_params=pltpu.CompilerParams(
-            collective_id=0, has_side_effects=True, vmem_limit_bytes=VMEM_BUDGET),
+            collective_id=0, has_side_effects=True),
     )(block_count, norm_gain.reshape(1, rows), hidden_in, normed_grad, key_grad,
       weight_blocks.reshape(most, LANE))
     return hgrad, wgrad.reshape(1, 1, most, LANE)

time: 53.1 us -> 50.1 us (0.944); the launches traced: 52.1 us -> 49.9 us
  local copies, waits for them, and re-layouts: 6.73 us -> 2.63 us
  Pallas kernels: 44.8 us -> 46.6 us
    unnamed x14 -> x4, local copies, waits for them, and re-layouts: 6.73 us -> 2.63 us
    pallas_call x1, Pallas kernels: 44.8 us -> 46.6 us  [fast_shards(): pl.pallas_call(functools.partial(fast_kernel, dims, windows), out_shape=(...]
where the time goes in v3:
time: 50.1 us; the launch traced here: 49.9 us
  Pallas kernels  46.6 us (93%)
  local copies, waits for them, and re-layouts  2.63 us (5%)
  between operations  0.65 us (1%)
    pallas_call x1, Pallas kernels, fast_shards(): pl.pallas_call(functools.partial(fast_kernel, dims, windows), out_shape=(...  46.6 us
    unnamed x4, local copies, waits for them, and re-layouts  2.63 us

profile of v3, /device:TPU:0, one launch (start us, length us, event | category | flops | bytes accessed | tf_op | source)
XLA Modules:
  0.0 49.9 jit_solution(16433674125220497243)
XLA Ops:
  0.6 46.6 %shard_map.77 = (bf16[128,2048]{1,0:T(8,128)(2,1)}, f32[520,128]{1,0:T(8,128)}) custom-call(s32[1,16]{1,0:T(1,128)} %count_ref.1, f32[1,2048]{1,0:T(1,128)} %bitcast.5, bf16[128,2048]{1,0:T(8,128)(2,1)} %hidden_hbm.1, bf16[128,2048]{1,0:T(8,128)(2,1)} %ngrad_hbm.1, bf16[128,512]{1,0:T(8,128)(2,1)} %key_hbm.1, bf16[520,128]{1,0:T(8,128)(2,1)} %bitcast.4), custom_call_target="tpu_custom_call" | custom-call | tf_op jit(solution)/shard_map/pallas_call | solution.py:344
  47.2 0.0 copy-start
  47.2 1.9 %copy.10 = bf16[128,2048]{1,0:T(8,128)(2,1)} copy(bf16[128,2048]{1,0:T(8,128)(2,1)} %get-tuple-element.8) | data formatting | bytes 1048576
  49.2 0.0 copy-done
  49.2 0.7 %copy.11 = f32[1,1,520,128]{3,2,1,0:T(8,128)} copy(f32[1,1,520,128]{3,2,1,0:T(8,128)S(1)} %bitcast.3) | data formatting | bytes 532480
Async XLA Ops:
  47.2 1.9 %copy-start = (f32[520,128]{1,0:T(8,128)S(1)}, f32[520,128]{1,0:T(8,128)}, u32[]{:S(2)}) copy-start(f32[520,128]{1,0:T(8,128)} %get-tuple-element.5) | copy-start | bytes 798724

commit v4 on v1

--- a/solution.py
+++ b/solution.py
@@ -28,9 +28,9 @@
 
 def fast_kernel(
     dims, windows,
-    count_ref, hidden_ref, gain_ref, ngrad_ref, key_ref, wb_ref,
+    count_ref, hidden_hbm, gain_ref, ngrad_hbm, key_hbm, wb_hbm,
     hgrad_ref, wgrad_ref,
-    kall, nt_send, nt_recv, pt_send, pt_recv, feat, wpad, wflat, wwin, dacc, dflat,
+    hidden_ref, ngrad_ref, wb_ref, kall, nt_send, nt_recv, pt_send, pt_recv, feat, wpad, wflat, wwin, dacc, dflat,
     sq_send, sq_recv, pj_send, pj_recv,
     own_sem, z_send, z_recv, s1_send, s1_recv, s2_send, s2_recv, s3_send, s3_recv,
     n_send, n_recv, p_send, p_recv, e_send, e_recv,
@@ -56,6 +56,16 @@
             src_ref=src, dst_ref=dst, send_sem=send, recv_sem=recv,
             device_id=(gx, gy, gz), device_id_type=MESH)
 
+    own = [pltpu.make_async_copy(key_hbm.at[pl.ds(h * half, half)], kall.at[a, c, h, x], own_sem.at[h])
+           for h in range(2)]
+    own += [
+        pltpu.make_async_copy(hidden_hbm, hidden_ref, own_sem.at[2]),
+        pltpu.make_async_copy(wb_hbm, wb_ref, own_sem.at[3]),
+        pltpu.make_async_copy(ngrad_hbm, ngrad_ref, own_sem.at[4]),
+    ]
+    for copy in own:
+        copy.start()
+
     pairs = [(rel, k) for rel in range(outer) for k in range(inner) if rel or k]
     barrier = pltpu.get_barrier_semaphore()
     for rel, k in pairs:
@@ -63,18 +73,7 @@
         pl.semaphore_signal(barrier, inc=1, device_id=(pa, px * 2 + pc, g), device_id_type=MESH)
     pl.semaphore_signal(barrier, inc=1, device_id=(a, b, og), device_id_type=MESH)
 
-    own = [pltpu.make_async_copy(key_ref.at[pl.ds(h * half, half)], kall.at[a, c, h, x], own_sem.at[h])
-           for h in range(2)]
-    for copy in own:
-        copy.start()
-
-    squares = jnp.zeros((tokens, LANE), f32)
-    for i in range(chunks):
-        part = hidden_ref[:, i * LANE:(i + 1) * LANE].astype(f32)
-        squares = squares + part * part
-    row_sum = jnp.sum(squares, axis=1, keepdims=True)
-    sq_send[...] = jnp.broadcast_to(row_sum, (tokens, LANE)).T[0:8, :]
-    for copy in own:
+    for copy in own[0:2]:
         copy.wait()
     pl.semaphore_wait(barrier, owners)
 
@@ -85,7 +84,6 @@
         sends.append(copy)
         return copy
 
-    sq_copy = start(remote(sq_send, sq_recv, e_send.at[0], e_recv.at[0], a, b, og))
     zc = {}
     for rel in range(1, outer):
         piece = kall.at[a, c, g, x]
@@ -95,6 +93,14 @@
     own_piece = kall.at[a, c, g, x]
     step1 = {0: start(remote(own_piece, own_piece, s1_send.at[0], s1_recv.at[0], a, bx, g))}
     step2, step3 = {}, {}
+    own[2].wait()
+    squares = jnp.zeros((tokens, LANE), f32)
+    for i in range(chunks):
+        part = hidden_ref[:, i * LANE:(i + 1) * LANE].astype(f32)
+        squares = squares + part * part
+    row_sum = jnp.sum(squares, axis=1, keepdims=True)
+    sq_send[...] = jnp.broadcast_to(row_sum, (tokens, LANE)).T[0:8, :]
+    sq_copy = start(remote(sq_send, sq_recv, e_send.at[0], e_recv.at[0], a, b, og))
 
     begin = jnp.int32(0)
     window_low = jnp.int32(0)
@@ -108,6 +114,7 @@
     flat_rows = height * per_row
     slot = lax.broadcasted_iota(jnp.int32, (most, LANE), 0)
     wpad[...] = jnp.zeros_like(wpad)
+    own[3].wait()
     wpad[pad:pad + most, :] = jnp.where(slot < count, wb_ref[...].astype(f32), 0.0)
     wflat[...] = wpad[pl.ds(pad - offset, flat_rows), :]
     for i in range(per_row):
@@ -193,6 +200,7 @@
 
     for rel, k in pairs:
         pc_copies[rel, k].wait_recv()
+    own[4].wait()
     feat[...] = jnp.zeros_like(feat)
     for o in range(owners):
         feat[windows[o]:windows[o] + height, :] += pt_recv[o].astype(f32)
@@ -247,12 +255,14 @@
     f32, bf16 = jnp.float32, jnp.bfloat16
     vmem, dma = pltpu.VMEM, pltpu.SemaphoreType.DMA
     in_vmem = pl.BlockSpec(memory_space=pltpu.VMEM)
+    in_hbm = pl.BlockSpec(memory_space=pltpu.HBM)
     hgrad, wgrad = pl.pallas_call(
         functools.partial(fast_kernel, dims, windows),
         out_shape=(jax.ShapeDtypeStruct((tokens, rows), bf16), jax.ShapeDtypeStruct((most, LANE), f32)),
-        in_specs=[pl.BlockSpec(memory_space=pltpu.SMEM)] + [in_vmem] * 5,
+        in_specs=[pl.BlockSpec(memory_space=pltpu.SMEM), in_hbm, in_vmem] + [in_hbm] * 3,
         out_specs=(in_vmem, in_vmem),
         scratch_shapes=[
+            vmem((tokens, rows), bf16), vmem((tokens, rows), bf16), vmem((most, LANE), bf16),
             vmem((outer, 2, 2, 2, tokens // 2, width), bf16),
             vmem((owners, height, tokens), bf16), vmem((owners, height, tokens), bf16),
             vmem((owners, height, tokens), bf16), vmem((owners, height, tokens), bf16),
@@ -260,10 +270,10 @@
             vmem((pad + max(flat_rows, most), LANE), f32), vmem((flat_rows, LANE), f32),
             vmem((height, width), bf16), vmem((height, width), f32), vmem((flat_rows + most, LANE), f32),
             vmem((8, LANE), f32), vmem((8, LANE), f32), vmem((8, LANE), f32), vmem((8, LANE), f32),
-            dma((2,)),
+            dma((5,)),
         ] + [dma((outer,))] * 8 + [dma((owners,))] * 4 + [dma((2,))] * 2,
         compiler_params=pltpu.CompilerParams(
-            collective_id=0, has_side_effects=True, vmem_limit_bytes=VMEM_BUDGET),
+            collective_id=0, has_side_effects=True),
     )(block_count, hidden_in, norm_gain.reshape(1, rows), normed_grad, key_grad,
       weight_blocks.reshape(most, LANE))
     return hgrad, wgrad.reshape(1, 1, most, LANE)

time: 49.3 us -> 46.2 us (0.937)
  local copies, waits for them, and re-layouts: 6.73 us -> 2.63 us
  Pallas kernels: 41.6 us -> 42.7 us
    unnamed x14 -> x4, local copies, waits for them, and re-layouts: 6.73 us -> 2.63 us
    pallas_call x1, Pallas kernels: 41.6 us -> 42.7 us  [fast_shards(): pl.pallas_call(functools.partial(fast_kernel, dims, windows), out_shape=(...]
where the time goes in v4:
time: 46.2 us; the launch traced here: 46 us
  Pallas kernels  42.7 us (92%)
  local copies, waits for them, and re-layouts  2.63 us (6%)
  between operations  0.65 us (1%)
    pallas_call x1, Pallas kernels, fast_shards(): pl.pallas_call(functools.partial(fast_kernel, dims, windows), out_shape=(...  42.7 us
    unnamed x4, local copies, waits for them, and re-layouts  2.63 us

profile of v4, /device:TPU:24, one launch (start us, length us, event | category | flops | bytes accessed | tf_op | source)
XLA Modules:
  0.0 46.0 jit_solution(8907527140731772550)
XLA Ops:
  0.6 42.7 %shard_map.77 = (bf16[128,2048]{1,0:T(8,128)(2,1)}, f32[520,128]{1,0:T(8,128)}) custom-call(s32[1,16]{1,0:T(1,128)} %count_ref.1, bf16[128,2048]{1,0:T(8,128)(2,1)} %hidden_hbm.1, f32[1,2048]{1,0:T(1,128)} %bitcast.5, bf16[128,2048]{1,0:T(8,128)(2,1)} %ngrad_hbm.1, bf16[128,512]{1,0:T(8,128)(2,1)} %key_hbm.1, bf16[520,128]{1,0:T(8,128)(2,1)} %bitcast.4), custom_call_target="tpu_custom_call" | custom-call | tf_op jit(solution)/shard_map/pallas_call | solution.py:259
  43.3 0.0 copy-start
  43.3 1.9 %copy.10 = bf16[128,2048]{1,0:T(8,128)(2,1)} copy(bf16[128,2048]{1,0:T(8,128)(2,1)} %get-tuple-element.8) | data formatting | bytes 1048576
  45.2 0.0 copy-done
  45.2 0.7 %copy.11 = f32[1,1,520,128]{3,2,1,0:T(8,128)} copy(f32[1,1,520,128]{3,2,1,0:T(8,128)S(1)} %bitcast.3) | data formatting | bytes 532480
Async XLA Ops:
  43.3 1.9 %copy-start = (f32[520,128]{1,0:T(8,128)S(1)}, f32[520,128]{1,0:T(8,128)}, u32[]{:S(2)}) copy-start(f32[520,128]{1,0:T(8,128)} %get-tuple-element.5) | copy-start | bytes 798724
